TPU v7x, 8 devices: a whole 2x2x1 slice. The times are simulated.
8 devices in a mesh: dp: 1 (over z), tp: 8 (over y, x, core).
Axes of the slice: x: 2, y: 2, z: 1, core: 2. Of those that a mesh axis runs over, the one named last changes fastest.
Arguments:
- x_in: bfloat16 [2, 2048, 1152], P('dp', 'tp')
- y_text: bfloat16 [2, 120, 1152], P('dp', 'tp')
- t_emb: bfloat16 [2, 6912], P('dp')
- text_len: int32 [2], P('dp')
- mod_table: bfloat16 [6, 1152], replicated
- w_qkv: bfloat16 [1152, 16, 216], P(None, 'tp')
- b_qkv: bfloat16 [16, 216], P('tp')
- w_o: bfloat16 [16, 72, 1152], P('tp')
- b_o: bfloat16 [1152], replicated
- w_q: bfloat16 [1152, 16, 72], P(None, 'tp')
- b_q: bfloat16 [16, 72], P('tp')
- w_kv: bfloat16 [1152, 16, 144], P(None, 'tp')
- b_kv: bfloat16 [16, 144], P('tp')
- w_co: bfloat16 [16, 72, 1152], P('tp')
- b_co: bfloat16 [1152], replicated
- w_1: bfloat16 [1152, 4608], P(None, 'tp')
- b_1: bfloat16 [4608], P('tp')
- w_2: bfloat16 [4608, 1152], P('tp')
- b_2: bfloat16 [1152], replicated
- g_out: bfloat16 [2, 2048, 1152], P('dp', 'tp')
Outputs:
- output 1: bfloat16 [2, 2048, 1152], P('dp', 'tp')
- output 2: bfloat16 [2, 2048, 1152], P('dp', 'tp')
- output 3: bfloat16 [2, 120, 1152], P('dp', 'tp')
- output 4: float32 [6, 1152], P('dp')
- output 5: bfloat16 [1152, 16, 216], P('dp', 'tp')
- output 6: bfloat16 [16, 216], P(('dp', 'tp'))
- output 7: bfloat16 [16, 72, 1152], P(('dp', 'tp'))
- output 8: bfloat16 [1152], P('dp')
- output 9: bfloat16 [1152, 16, 72], P('dp', 'tp')
- output 10: bfloat16 [16, 72], P(('dp', 'tp'))
- output 11: bfloat16 [1152, 16, 144], P('dp', 'tp')
- output 12: bfloat16 [16, 144], P(('dp', 'tp'))
- output 13: bfloat16 [16, 72, 1152], P(('dp', 'tp'))
- output 14: bfloat16 [1152], P('dp')
- output 15: bfloat16 [1152, 4608], P('dp', 'tp')
- output 16: bfloat16 [4608], P(('dp', 'tp'))
- output 17: bfloat16 [4608, 1152], P(('dp', 'tp'))
- output 18: bfloat16 [1152], P('dp')
All inputs are finite; a program needn't handle non-finite values.
Results may differ from a plain program's by a relative error of at most 0.0195586.
Values are sent between devices in bfloat16 or wider.
A program may use at most 1 GiB of HBM per device.

v0:
```python
import functools
import math

import jax
import jax.numpy as jnp
from jax import lax
from jax.experimental import pallas as pl
from jax.experimental.pallas import tpu as pltpu
from jax.sharding import PartitionSpec as P


LN_EPS = 1e-6
MASK_FILL = -1e30
N_DEV = 8
TP = ('y', 'x', 'c')
ROW = ('x', 'c')
UNROLL = 1
LOG2E = math.log2(math.e)
BF = jnp.bfloat16
F32 = jnp.float32


def product(form, lhs, rhs):
    return jnp.einsum(form, lhs, rhs, preferred_element_type=F32)


def layer_norm(tensor):
    tensor = tensor.astype(F32)
    centered = tensor - jnp.mean(tensor, axis=-1, keepdims=True)
    inv_std = lax.rsqrt(jnp.mean(centered * centered, axis=-1, keepdims=True) + LN_EPS)
    return centered * inv_std, inv_std


def layer_norm_back(normed, inv_std, g_normed):
    mean_g = jnp.mean(g_normed, axis=-1, keepdims=True)
    mean_gn = jnp.mean(g_normed * normed, axis=-1, keepdims=True)
    return inv_std * (g_normed - mean_g - normed * mean_gn)


def gelu_tanh(tensor):
    return jax.nn.gelu(tensor, approximate=True)


def dot00(lhs, rhs):
    return lax.dot_general(lhs, rhs, (((0,), (0,)), ((), ())), preferred_element_type=F32)


def dot10(lhs, rhs):
    return lax.dot_general(lhs, rhs, (((1,), (0,)), ((), ())), preferred_element_type=F32)


def dot11(lhs, rhs):
    return lax.dot_general(lhs, rhs, (((1,), (1,)), ((), ())), preferred_element_type=F32)


def my_index():
    return lax.axis_index('y') * 4 + lax.axis_index('x') * 2 + lax.axis_index('c')


def device(index):
    return {'y': index // 4, 'x': (index // 2) % 2, 'c': index % 2}


def entry_barrier(me):
    barrier = pltpu.get_barrier_semaphore()
    for k in range(1, N_DEV):
        pl.semaphore_signal(barrier, inc=1, device_id=device(me ^ k), device_id_type=pl.DeviceIdType.MESH)
    pl.semaphore_wait(barrier, N_DEV - 1)


def block_copy(src, dst, send_sem, recv_sem, peer, k):
    if k == 0:
        return pltpu.make_async_copy(src, dst, recv_sem)
    return pltpu.make_async_remote_copy(src_ref=src, dst_ref=dst, send_sem=send_sem, recv_sem=recv_sem, device_id=device(peer), device_id_type=pl.DeviceIdType.MESH)


def start_all(copies):
    for copy in copies:
        copy.start()


def wait_all(copies):
    for copy in copies:
        copy.wait()


def block_at(index, blk):
    return pl.ds(pl.multiple_of(index * blk, blk), blk)


def attn_fwd_kernel(scale, blk, heads, qkv_ref, kv_ref, o_ref, lse_ref, tok_ref, kv_out, o_scr, send, recv, kv_send, kv_recv):
    i = pl.program_id(0)
    last = pl.num_programs(0) - 1
    tokens = o_ref.shape[2]
    factor = scale * LOG2E
    me = my_index()

    def o_copies(step):
        return [block_copy(o_scr.at[step, :, block_at(me ^ k, blk)], tok_ref.at[step // heads, me * heads + step % heads], send.at[step, k], recv.at[step, k], me ^ k, k) for k in range(N_DEV)]

    kv_copies = [block_copy(kv_ref, kv_out.at[me], kv_send.at[k], kv_recv.at[k], me ^ k, k) for k in range(N_DEV)]

    @pl.when(i == 0)
    def _():
        entry_barrier(me)
        start_all(kv_copies)

    def step(j, carry):
        cols = block_at(j, blk)
        s = dot00(qkv_ref[0, 1], qkv_ref[0, 0, :, cols])
        top = jnp.max(s, axis=0, keepdims=True) * factor
        p = jnp.exp2(s * factor - top)
        total = jnp.sum(p, axis=0, keepdims=True)
        o = dot10(qkv_ref[0, 2], p.astype(BF))
        o_scr[i, :, cols] = (o / total).astype(BF)
        lse_ref[0, :, cols] = top + jnp.log2(total)
        return carry

    lax.fori_loop(0, tokens // blk, step, 0, unroll=UNROLL)
    o_ref[0] = o_scr[i]
    start_all(o_copies(i))

    @pl.when(i == last)
    def _():
        for n in range(o_scr.shape[0]):
            wait_all(o_copies(n))
        wait_all(kv_copies)


def attn_fwd(qkv, kv, heads, blk):
    steps, _, hd, tokens = qkv.shape
    batch = steps // heads
    hbm = pl.BlockSpec(memory_space=pl.ANY)
    dma = pltpu.SemaphoreType.DMA
    return pl.pallas_call(
        functools.partial(attn_fwd_kernel, hd ** -0.5, blk, heads),
        grid=(steps,),
        in_specs=[pl.BlockSpec((1, 3, hd, tokens), lambda i: (i, 0, 0, 0)), hbm],
        out_specs=[pl.BlockSpec((1, hd, tokens), lambda i: (i, 0, 0)), pl.BlockSpec((1, 1, tokens), lambda i: (i, 0, 0)), hbm, hbm],
        out_shape=[jax.ShapeDtypeStruct((steps, hd, tokens), BF), jax.ShapeDtypeStruct((steps, 1, tokens), F32),
                   jax.ShapeDtypeStruct((batch, N_DEV * heads, hd, blk), BF), jax.ShapeDtypeStruct((N_DEV,) + kv.shape, BF)],
        scratch_shapes=[pltpu.VMEM((steps, hd, tokens), BF), dma((steps, N_DEV)), dma((steps, N_DEV)), dma((N_DEV,)), dma((N_DEV,))],
        cost_estimate=pl.CostEstimate(flops=4 * steps * hd * tokens * tokens, bytes_accessed=steps * hd * tokens * 8, transcendentals=steps * tokens * tokens),
        compiler_params=pltpu.CompilerParams(collective_id=1, has_side_effects=True, vmem_limit_bytes=48 << 20),
        name="attn_fwd",
    )(qkv, kv)


def attn_bwd_kernel(scale, blk, heads, qkv_ref, o_ref, lse_ref, g_ref, *refs):
    rows, (d_ref, tok_ref, early_out, g_scr, d_scr, early_scr, dk_acc, dv_acc, g_send, g_recv, d_send, d_recv, x_send, x_recv) = refs[:-14], refs[-14:]
    i = pl.program_id(0)
    steps = d_scr.shape[0]
    tokens = o_ref.shape[2]
    factor = scale * LOG2E
    me = my_index()

    def g_copies(step):
        return [block_copy(g_ref.at[step // heads, (me ^ k) * heads + step % heads], g_scr.at[step, :, block_at(me, blk)], g_send.at[step, k], g_recv.at[step, k], me ^ k, k) for k in range(N_DEV)]

    def d_copies(step):
        return [block_copy(d_scr.at[step, :, :, block_at(me ^ k, blk)], tok_ref.at[step // heads, me * heads + step % heads], d_send.at[step, k], d_recv.at[step, k], me ^ k, k) for k in range(N_DEV)]

    x_copies = [block_copy(early_scr, early_out.at[me], x_send.at[k], x_recv.at[k], me ^ k, k) for k in range(N_DEV)]

    @pl.when(i == 0)
    def _():
        entry_barrier(me)
        for n in range(steps):
            start_all(g_copies(n))
        early_scr[...] = jnp.zeros_like(early_scr)
        place = 0
        for row in rows:
            early_scr[place:place + row.shape[0], :] = row[...]
            place += row.shape[0]

    wait_all(g_copies(i))
    dk_acc[...] = jnp.zeros_like(dk_acc)
    dv_acc[...] = jnp.zeros_like(dv_acc)

    def step(j, carry):
        cols = block_at(j, blk)
        q = qkv_ref[0, 0, :, cols]
        g = g_scr[i, :, cols]
        delta = jnp.sum(g.astype(F32) * o_ref[0, :, cols].astype(F32), axis=0, keepdims=True)
        s = dot00(qkv_ref[0, 1], q)
        p = jnp.exp2(s * factor - lse_ref[0, :, cols])
        dp = dot00(qkv_ref[0, 2], g)
        ds = (p * (dp - delta)).astype(BF)
        dv_acc[...] += dot11(g, p.astype(BF))
        dk_acc[...] += dot11(q, ds)
        d_scr[i, 0, :, cols] = (dot10(qkv_ref[0, 1], ds) * scale).astype(BF)
        return carry

    lax.fori_loop(0, tokens // blk, step, 0, unroll=UNROLL)
    d_scr[i, 1] = (dk_acc[...] * scale).astype(BF)
    d_scr[i, 2] = dv_acc[...].astype(BF)
    d_ref[0] = d_scr[i]
    start_all(d_copies(i))

    @pl.when(i == 0)
    def _():
        start_all(x_copies)

    @pl.when(i == steps - 1)
    def _():
        for n in range(steps):
            wait_all(d_copies(n))
        wait_all(x_copies)


def attn_bwd(qkv, o, lse, g, early, heads, blk):
    steps, _, hd, tokens = qkv.shape
    batch = steps // heads
    hbm = pl.BlockSpec(memory_space=pl.ANY)
    dma = pltpu.SemaphoreType.DMA
    row = lambda i: (i, 0, 0)
    return pl.pallas_call(
        functools.partial(attn_bwd_kernel, hd ** -0.5, blk, heads),
        grid=(steps,),
        in_specs=[pl.BlockSpec((1, 3, hd, tokens), lambda i: (i, 0, 0, 0)), pl.BlockSpec((1, hd, tokens), row), pl.BlockSpec((1, 1, tokens), row), hbm] + [pl.BlockSpec(part.shape, lambda i: (0, 0)) for part in early],
        out_specs=[pl.BlockSpec((1, 3, hd, tokens), lambda i: (i, 0, 0, 0)), hbm, hbm],
        out_shape=[jax.ShapeDtypeStruct(qkv.shape, BF), jax.ShapeDtypeStruct((batch, N_DEV * heads, 3, hd, blk), BF),
                   jax.ShapeDtypeStruct((N_DEV, 16, early[0].shape[1]), F32)],
        scratch_shapes=[pltpu.VMEM((steps, hd, tokens), BF), pltpu.VMEM(qkv.shape, BF), pltpu.VMEM((16, early[0].shape[1]), F32), pltpu.VMEM((hd, tokens), F32), pltpu.VMEM((hd, tokens), F32),
                        dma((steps, N_DEV)), dma((steps, N_DEV)), dma((steps, N_DEV)), dma((steps, N_DEV)), dma((N_DEV,)), dma((N_DEV,))],
        cost_estimate=pl.CostEstimate(flops=10 * steps * hd * tokens * tokens, bytes_accessed=steps * hd * tokens * 20, transcendentals=steps * tokens * tokens),
        compiler_params=pltpu.CompilerParams(collective_id=2, has_side_effects=True, vmem_limit_bytes=56 << 20),
        name="attn_bwd",
    )(qkv, o, lse, g, *early)


def qkv_kernel(w_ref, b_ref, h_ref, out_ref):
    out_ref[0] = (dot11(w_ref[...], h_ref[0]) + b_ref[...]).astype(BF)


def qkv_project(w, bias, first, batch, blk):
    rows, width = w.shape
    return pl.pallas_call(
        qkv_kernel,
        grid=(batch, N_DEV),
        in_specs=[pl.BlockSpec((rows, width), lambda b, j: (0, 0)), pl.BlockSpec((rows, 1), lambda b, j: (0, 0)), pl.BlockSpec((1, blk, width), lambda b, j: (j, b, 0))],
        out_specs=pl.BlockSpec((1, rows, blk), lambda b, j: (b, 0, j)),
        out_shape=jax.ShapeDtypeStruct((batch, rows, N_DEV * blk), BF),
        cost_estimate=pl.CostEstimate(flops=2 * rows * width * batch * N_DEV * blk, bytes_accessed=2 * batch * N_DEV * blk * (rows + width), transcendentals=0),
        compiler_params=pltpu.CompilerParams(vmem_limit_bytes=24 << 20),
        name="qkv_project",
    )(w, bias, first)


def qkv_grad_kernel(g_ref, h_ref, parts, whole, w_ref, b_ref, parts_out, whole_out, w_acc, b_acc, send, recv):
    n = pl.program_id(0)
    me = my_index()
    copies = []
    for k in range(N_DEV):
        copies.append(block_copy(whole, whole_out.at[me], send.at[0, k], recv.at[0, k], me ^ k, k))
        copies.append(block_copy(parts.at[me ^ k], parts_out.at[me], send.at[1, k], recv.at[1, k], me ^ k, k))

    @pl.when(n == 0)
    def _():
        entry_barrier(me)
        start_all(copies)
        w_acc[...] = jnp.zeros_like(w_acc)
        b_acc[...] = jnp.zeros_like(b_acc)

    g = g_ref[0]
    w_acc[...] += dot10(g, h_ref[0])
    b_acc[...] += g.astype(F32)

    @pl.when(n == pl.num_programs(0) - 1)
    def _():
        w_ref[...] = w_acc[...].astype(BF)
        b_ref[...] = jnp.sum(b_acc[...], axis=1, keepdims=True)
        wait_all(copies)


def qkv_grad(g, first, parts, whole, blk):
    batch, rows, tokens = g.shape
    width = first.shape[2]
    hbm = pl.BlockSpec(memory_space=pl.ANY)
    dma = pltpu.SemaphoreType.DMA
    return pl.pallas_call(
        qkv_grad_kernel,
        grid=(batch * N_DEV,),
        in_specs=[pl.BlockSpec((1, rows, blk), lambda n: (n // N_DEV, 0, n % N_DEV)), pl.BlockSpec((1, blk, width), lambda n: (n % N_DEV, n // N_DEV, 0)), hbm, hbm],
        out_specs=[pl.BlockSpec((rows, width), lambda n: (0, 0)), pl.BlockSpec((rows, 1), lambda n: (0, 0)), hbm, hbm],
        out_shape=[jax.ShapeDtypeStruct((rows, width), BF), jax.ShapeDtypeStruct((rows, 1), F32),
                   jax.ShapeDtypeStruct(parts.shape, parts.dtype), jax.ShapeDtypeStruct((N_DEV,) + whole.shape, whole.dtype)],
        scratch_shapes=[pltpu.VMEM((rows, width), F32), pltpu.VMEM((rows, blk), F32), dma((2, N_DEV)), dma((2, N_DEV))],
        cost_estimate=pl.CostEstimate(flops=2 * rows * width * batch * tokens, bytes_accessed=2 * batch * tokens * (rows + width), transcendentals=0),
        compiler_params=pltpu.CompilerParams(collective_id=3, has_side_effects=True, vmem_limit_bytes=24 << 20),
        name="qkv_grad",
    )(g, first, parts, whole)


def cross_fwd_kernel(scale, len_ref, q_ref, kv_ref, c_ref, p_ref):
    heads, slots = q_ref.shape[1], kv_ref.shape[5]
    blk = q_ref.shape[3]
    count = len_ref[pl.program_id(0)]
    ok = lax.broadcasted_iota(jnp.int32, (slots, blk), 0) < count
    for h in range(heads):
        s = dot00(kv_ref[h // 2, 0, h % 2, 0], q_ref[0, h]) * scale
        s = jnp.where(ok, s, MASK_FILL)
        p = jnp.exp(s - jnp.max(s, axis=0, keepdims=True))
        p = (p / jnp.sum(p, axis=0, keepdims=True)).astype(BF)
        p_ref[0, h] = p
        c_ref[0, h] = dot10(kv_ref[h // 2, 0, h % 2, 1], p).astype(BF)


def cross_specs(hd, blk, slots, per):
    q_spec = pl.BlockSpec((1, per, hd, blk), lambda b, i, n: (b, i, 0, 0))
    kv_spec = pl.BlockSpec((per // 2, 1, 2, 2, hd, slots), lambda b, i, n: (i, b, 0, 0, 0, 0))
    p_spec = pl.BlockSpec((1, per, slots, blk), lambda b, i, n: (b, i, 0, 0))
    return q_spec, kv_spec, p_spec


def cross_fwd(lens, q, kv, per=8):
    batch, heads, hd, blk = q.shape
    slots = kv.shape[5]
    q_spec, kv_spec, p_spec = cross_specs(hd, blk, slots, per)
    return pl.pallas_call(
        functools.partial(cross_fwd_kernel, hd ** -0.5),
        grid_spec=pltpu.PrefetchScalarGridSpec(num_scalar_prefetch=1, grid=(batch, heads // per), in_specs=[q_spec, kv_spec], out_specs=[q_spec, p_spec]),
        out_shape=[jax.ShapeDtypeStruct(q.shape, BF), jax.ShapeDtypeStruct((batch, heads, slots, blk), BF)],
        cost_estimate=pl.CostEstimate(flops=4 * batch * heads * hd * blk * slots * 8, bytes_accessed=batch * heads * blk * (hd * 4 + slots * 2), transcendentals=batch * heads * blk * slots),
        compiler_params=pltpu.CompilerParams(vmem_limit_bytes=32 << 20),
        name="cross_fwd",
    )(lens, q, kv)


def cross_bwd_kernel(scale, len_ref, q_ref, kv_ref, p_ref, g_ref, gq_ref, gkv_ref):
    heads = q_ref.shape[1]
    for h in range(heads):
        k, v = kv_ref[h // 2, 0, h % 2, 0], kv_ref[h // 2, 0, h % 2, 1]
        q, g, p = q_ref[0, h], g_ref[0, h], p_ref[0, h]
        dp = dot00(v, g)
        pf = p.astype(F32)
        delta = jnp.sum(dp * pf, axis=0, keepdims=True)
        ds = (pf * (dp - delta) * scale).astype(BF)
        gq_ref[0, h] = dot10(k, ds).astype(BF)
        gkv_ref[h // 2, 0, h % 2, 0] = dot11(q, ds).astype(BF)
        gkv_ref[h // 2, 0, h % 2, 1] = dot11(g, p).astype(BF)


def cross_bwd(lens, q, kv, prob, g, per=8):
    batch, heads, hd, blk = q.shape
    slots = kv.shape[5]
    q_spec, kv_spec, p_spec = cross_specs(hd, blk, slots, per)
    return pl.pallas_call(
        functools.partial(cross_bwd_kernel, hd ** -0.5),
        grid_spec=pltpu.PrefetchScalarGridSpec(num_scalar_prefetch=1, grid=(batch, heads // per), in_specs=[q_spec, kv_spec, p_spec, q_spec], out_specs=[q_spec, kv_spec]),
        out_shape=[jax.ShapeDtypeStruct(q.shape, BF), jax.ShapeDtypeStruct(kv.shape, BF)],
        cost_estimate=pl.CostEstimate(flops=8 * batch * heads * hd * blk * slots * 8, bytes_accessed=batch * heads * blk * (hd * 6 + slots * 2), transcendentals=0),
        compiler_params=pltpu.CompilerParams(vmem_limit_bytes=32 << 20),
        name="cross_bwd",
    )(lens, q, kv, prob, g)


def gather_rows(tensor, axes=TP):
    return lax.all_gather(tensor, axes, axis=0, tiled=True)


def scatter_rows(tensor, axes=TP):
    return lax.psum_scatter(tensor.astype(BF), axes, scatter_dimension=0, tiled=True)


def swap(tensor, axis):
    return lax.ppermute(tensor, axis, [(0, 1), (1, 0)])


def swap_y(tensor):
    return swap(tensor, 'y')


def row_reduce(rows):
    grid = rows.reshape(2, 2, -1, rows.shape[1])
    core = lax.axis_index('c')
    other = swap(lax.dynamic_index_in_dim(grid, 1 - core, 1, keepdims=False), 'c')
    return (lax.dynamic_index_in_dim(grid, core, 1, keepdims=False).astype(F32) + other.astype(F32)).astype(BF)


def row_finish(pair):
    place = lax.axis_index('x')
    other = swap(lax.dynamic_index_in_dim(pair, 1 - place, 0, keepdims=False), 'x')
    return (lax.dynamic_index_in_dim(pair, place, 0, keepdims=False).astype(F32) + other.astype(F32)).astype(BF)


def mlp_hidden(h2, w1_half, b1_half):
    hidden = product('btd,fd->btf', h2, w1_half) + b1_half
    gelu_out, gelu_vjp = jax.vjp(gelu_tanh, hidden)
    return gelu_out.astype(BF), gelu_vjp


def mlp_rest(gelu_out, gelu_vjp, g_mlp, w1_half, w2_half, name):
    g_hidden = gelu_vjp(product('btd,fd->btf', g_mlp, w2_half))[0]
    g_b_1 = jnp.sum(g_hidden, axis=(0, 1))
    g_hidden = g_hidden.astype(BF)
    g_h2 = product('btf,fd->btd', g_hidden, w1_half)
    part = product('btf,fd->btd', gelu_out, w2_half)
    part = part if name == 'own' else part.astype(BF)
    return gelu_out, part, g_hidden, g_b_1, g_h2


def device_block(x_loc, y_loc, t_loc, len_loc, mod_table, w_qkv, b_qkv, w_o, b_o, w_q, b_q, w_kv, b_kv, w_co, b_co, w_1, b_1, w_2, b_2, g_loc):
    batch, n_loc, width = x_loc.shape
    heads_loc, head_dim = w_q.shape[1], w_q.shape[2]
    heads = heads_loc * N_DEV
    inner = heads * head_dim
    slots_loc = y_loc.shape[1]
    slots = slots_loc * N_DEV
    slots_pad = 128
    ffn_loc = w_1.shape[1]
    ffn = ffn_loc * N_DEV
    mod_rows = mod_table.astype(F32)[None] + t_loc.astype(F32).reshape(batch, 6, width)
    shift1, scale1, gate1, shift2, scale2, gate2 = [mod_rows[:, row_idx, None, :] for row_idx in range(6)]

    g_x2 = g_loc.astype(F32)
    g_mlp_f = g_x2 * gate2
    g_b_2 = jnp.sum(g_mlp_f, axis=(0, 1))
    g_mlp = g_mlp_f.astype(BF)

    normed1, inv_std1 = layer_norm(x_loc)
    h1 = (normed1 * (1.0 + scale1) + shift1).astype(BF)

    rows_loc = heads_loc * head_dim
    wqkv_t = w_qkv.transpose(1, 2, 0)
    wkv_t = w_kv.transpose(1, 2, 0)
    wq_t = w_q.transpose(1, 2, 0).reshape(rows_loc, width)
    small = jnp.concatenate([b_q.reshape(-1), b_1])
    small = jnp.pad(small, (0, width - small.shape[0]))[None]
    n_rows = batch * n_loc
    n_text = batch * slots_loc
    first = jnp.concatenate([h1.reshape(n_rows, width), y_loc.reshape(n_text, width), small, jnp.zeros((31 - n_text, width), BF)], axis=0)
    first = gather_rows(first[None])
    y_all = first[:, n_rows:n_rows + n_text].reshape(N_DEV, batch, slots_loc, width).transpose(1, 0, 2, 3).reshape(batch, slots, width)
    y_all = jnp.pad(y_all, ((0, 0), (0, slots_pad - slots), (0, 0)))
    small_all = first[:, n_rows + n_text]
    bq_all = small_all[:, :rows_loc].reshape(inner)
    b1_all = small_all[:, rows_loc:rows_loc + ffn_loc]
    b1_half = lax.dynamic_index_in_dim(b1_all.reshape(2, ffn // 2), lax.axis_index('y'), keepdims=False)
    square = jnp.concatenate([w_o.reshape(rows_loc, width), wq_t, w_co.reshape(rows_loc, width)], axis=0)
    square = gather_rows(square[None])
    w1_half = gather_rows(w_1.T, ROW)
    w2_half = gather_rows(w_2, ROW)
    wqkv_all = gather_rows(wqkv_t.reshape(heads_loc * 3 * head_dim, width))

    tokens = N_DEV * n_loc
    qkv_rows = heads_loc * 3 * head_dim
    qkv = qkv_project(wqkv_t.reshape(qkv_rows, width), b_qkv.astype(F32).reshape(qkv_rows, 1), first, batch, n_loc)
    qkv = qkv.reshape(batch * heads_loc, 3, head_dim, tokens)
    kv_t = (product('hed,bsd->bhes', wkv_t, y_all) + b_kv[None, :, :, None]).astype(BF)
    o_heads, lse, o_tok, kv_all = attn_fwd(qkv, kv_t.reshape(batch, heads_loc, 2, head_dim, slots_pad), heads_loc, n_loc)
    o_tok = o_tok.reshape(batch, inner, n_loc)
    square, o_tok, g_mlp = lax.optimization_barrier((square, o_tok, g_mlp))
    g_mlp_far = swap_y(g_mlp)
    wo_all, wq_all, wco_all = [square[:, n * rows_loc:(n + 1) * rows_loc].reshape(inner, width) for n in range(3)]

    attn_total = product('bet,ed->btd', o_tok, wo_all) + b_o
    x1 = (x_loc + gate1 * attn_total).astype(BF)
    q_cross = (product('ed,btd->bet', wq_all, x1) + bq_all[None, :, None]).astype(BF)
    q_cross = q_cross.reshape(batch, heads, head_dim, n_loc)
    cross_val, cross_prob = cross_fwd(len_loc, q_cross, kv_all)
    cross_rows = cross_val.reshape(batch, inner, n_loc)
    x2 = (x1 + (product('bet,ed->btd', cross_rows, wco_all) + b_co)).astype(BF)

    normed2, inv_std2 = layer_norm(x2)
    h2 = (normed2 * (1.0 + scale2) + shift2).astype(BF)
    gelu_own, vjp_own = mlp_hidden(h2, w1_half, b1_half)
    h2_far = swap_y(h2)
    gelu_far, vjp_far = mlp_hidden(h2_far, w1_half, b1_half)
    w2_half, gelu_own, gelu_far = lax.optimization_barrier((w2_half, gelu_own, gelu_far))
    own = mlp_rest(gelu_own, vjp_own, g_mlp, w1_half, w2_half, 'own')
    far = mlp_rest(gelu_far, vjp_far, g_mlp_far, w1_half, w2_half, 'far')
    g_h2_far, gelu_own, g_hid_own = far[4].astype(BF), own[0], own[2]
    g_h2_far = swap_y(g_h2_far)
    pair = lambda near, other: jnp.concatenate([near, other], axis=0)
    p_w_2 = product('btf,btd->fd', pair(gelu_own, far[0]), pair(g_mlp, g_mlp_far)).astype(BF)
    p_w_2 = row_reduce(p_w_2)
    p_w_1 = product('btf,btd->fd', pair(g_hid_own, far[2]), pair(h2, h2_far)).astype(BF)
    p_w_1 = row_reduce(p_w_1)
    part_own, part_far = own[1], far[1]
    g_h2_far, part_own, part_far, _, _ = lax.optimization_barrier((g_h2_far, part_own, part_far, p_w_2, p_w_1))
    g_h2 = own[4] + g_h2_far.astype(F32)
    part_far = swap_y(part_far)
    g_w_2 = row_finish(p_w_2)
    g_w_1 = row_finish(p_w_1).T
    g_b_1 = own[3] + far[3]
    g_shift2 = jnp.sum(g_h2, axis=(0, 1))
    g_scale2 = jnp.sum(g_h2 * normed2, axis=(0, 1))
    g_x2 = g_x2 + layer_norm_back(normed2, inv_std2, g_h2 * (1.0 + scale2))

    g_b_co = jnp.sum(g_x2, axis=(0, 1))
    g_cross = g_x2.astype(BF)
    p_w_co = product('bet,btd->ed', cross_rows, g_cross).astype(BF)
    g_cross_val = product('btd,ed->bet', g_cross, wco_all).astype(BF).reshape(batch, heads, head_dim, n_loc)
    g_cross_val, wqkv_all = lax.optimization_barrier((g_cross_val, wqkv_all))
    g_q, g_kv = cross_bwd(len_loc, q_cross, kv_all, cross_prob, g_cross_val)
    g_kv = scatter_rows(g_kv)
    g_q = g_q.reshape(batch, inner, n_loc)
    g_b_q = jnp.sum(g_q.astype(F32), axis=(0, 2))
    p_w_q = product('bet,btd->ed', g_q, x1).astype(BF)
    g_x1 = g_x2 + product('bet,ed->btd', g_q, wq_all)
    g_gate1 = jnp.sum(g_x1 * attn_total, axis=(0, 1))
    g_attn_f = g_x1 * gate1
    g_b_o = jnp.sum(g_attn_f, axis=(0, 1))
    g_attn = g_attn_f.astype(BF)
    p_w_o = product('bet,btd->ed', o_tok, g_attn).astype(BF)
    g_o = product('btd,ed->bet', g_attn, wo_all).astype(BF).reshape(batch, heads, head_dim, n_loc)
    g_w_co, g_w_q, g_w_o = scatter_rows(p_w_co), scatter_rows(p_w_q), scatter_rows(p_w_o)
    g_o, _, _, _ = lax.optimization_barrier((g_o, p_w_co, p_w_q, p_w_o))
    g_b_1 = jnp.where(lax.axis_index('y') == jnp.arange(2)[:, None], g_b_1[None], 0.0).reshape(ffn // width, width)
    early = [row[None] for row in (g_gate1, g_shift2, g_scale2, g_b_o, g_b_q, g_b_co, g_b_2)] + [g_b_1]
    g_qkv, g_qkv_tok, early = attn_bwd(qkv, o_heads, lse, g_o, early, heads_loc, n_loc)
    g_qkv_tok, part_far = lax.optimization_barrier((g_qkv_tok, part_far))
    g_kv, g_qkv_tok = lax.optimization_barrier((g_kv, g_qkv_tok))
    g_kv = g_kv.astype(F32).reshape(batch, heads_loc, 2 * head_dim, slots_pad)
    g_b_kv = jnp.sum(g_kv, axis=(0, 3))
    g_kv = g_kv.astype(BF)
    g_y = product('bhes,hed->bsd', g_kv, wkv_t)[:, :slots].astype(BF)
    g_y = g_y.reshape(batch, N_DEV, slots_loc, width).transpose(1, 0, 2, 3).reshape(N_DEV, n_text, width)
    g_y = jnp.pad(g_y, ((0, 0), (0, 32 - n_text), (0, 0)))
    g_w_kv = product('bhes,bsd->hed', g_kv, y_all).astype(BF).transpose(2, 0, 1)
    g_h1 = product('bet,ed->btd', g_qkv_tok.reshape(batch, 3 * inner, n_loc), wqkv_all)
    g_x = g_x1 + layer_norm_back(normed1, inv_std1, g_h1 * (1.0 + scale1))
    mlp_total = part_own + part_far.astype(F32) + b_2
    x_out = (x2 + gate2 * mlp_total).astype(BF)
    g_gate2 = jnp.sum(g_loc.astype(F32) * mlp_total, axis=(0, 1))
    late = jnp.stack([jnp.sum(g_h1, axis=(0, 1)), jnp.sum(g_h1 * normed1, axis=(0, 1)), g_gate2])
    late = jnp.pad(late, ((0, 5), (0, 0)))
    g_w_qkv, g_b_qkv, g_y, late = qkv_grad(g_qkv.reshape(batch, qkv_rows, tokens), first, g_y, late, n_loc)
    g_w_qkv = g_w_qkv.reshape(heads_loc, 3 * head_dim, width).transpose(2, 0, 1)
    g_b_qkv = g_b_qkv.reshape(heads_loc, 3 * head_dim)
    g_y = jnp.sum(g_y.astype(F32), axis=0)[:n_text].reshape(batch, slots_loc, width).astype(BF)
    late = jnp.sum(late, axis=0)
    early = jnp.sum(early, axis=0)
    me = my_index()
    g_b_q = lax.dynamic_slice(early[4], (me * heads_loc * head_dim,), (heads_loc * head_dim,)).reshape(heads_loc, head_dim)
    g_b_1 = lax.dynamic_slice(early[7:7 + ffn // width].reshape(ffn), (me * ffn_loc,), (ffn_loc,))

    return (x_out, g_x.astype(BF), g_y, jnp.concatenate([late[:2], early[:3], late[2:3]], axis=0), g_w_qkv, g_b_qkv.astype(BF), g_w_o.reshape(heads_loc, head_dim, width), early[3].astype(BF), g_w_q.reshape(heads_loc, head_dim, width).transpose(2, 0, 1), g_b_q.astype(BF), g_w_kv, g_b_kv.astype(BF), g_w_co.reshape(heads_loc, head_dim, width), early[5].astype(BF), g_w_1, g_b_1.astype(BF), g_w_2, early[6].astype(BF))


def solution(mesh):
    mesh = jax.sharding.Mesh(mesh.devices.reshape(-1, 2, 2, 2), ('dp',) + TP)
    token_spec = P('dp', TP, None)
    group_rows = ('dp',) + TP
    in_specs = (token_spec, token_spec, P('dp', None), P('dp'), P(None, None), P(None, TP, None), P(TP, None), P(TP, None, None), P(None), P(None, TP, None), P(TP, None), P(None, TP, None), P(TP, None), P(TP, None, None), P(None), P(None, TP), P(TP), P(TP, None), P(None), token_spec)
    out_specs = (token_spec, token_spec, token_spec, P('dp', None), P('dp', TP, None), P(group_rows, None), P(group_rows, None, None), P('dp'), P('dp', TP, None), P(group_rows, None), P('dp', TP, None), P(group_rows, None), P(group_rows, None, None), P('dp'), P('dp', TP), P(group_rows), P(group_rows, None), P('dp'))

    def step(*args):
        return device_block(*args)

    step = jax.shard_map(step, mesh=mesh, in_specs=in_specs, out_specs=out_specs, check_vma=False)
    return step
```

profile of v0, /device:TPU:0, one launch (start us, length us, event | category | flops | bytes accessed | tf_op | source)
XLA Modules:
  0.0 562.8 jit_solution(3902551322909546682)
XLA Ops:
  11.4 1.5 convert_reduce_fusion.1
  14.1 1.3 maximum_maximum_fusion
  15.6 1.0 pad_maximum_fusion
  18.3 1.3 fusion.68
  19.6 54.4 %all-gather.16.cloned.1.call-done = bf16[4352,1152]{1,0:T(8,128)(2,1)} async-done(((bf16[544,1152]{1,0:T(8,128)(2,1)}), bf16[4352,1152]{1,0:T(8,128)(2,1)}) %all-gather.16.cloned.1.call-update) | async-done | bytes 10027024 | tf_op jit(solution)/shard_map/all_gather | solution.py:359
  75.0 1.1 slice.100
  78.1 4.5 copy-done.4
  82.6 8.2 %qkv_project.1 = bf16[2,432,2048]{2,1,0:T(8,128)(2,1)S(1)} custom-call(bf16[432,1152]{1,0:T(8,128)(2,1)S(1)} %bitcast.225, f32[432,1]{1,0:T(8,128)S(1)} %reshape.312.b_ref, bf16[8,544,1152]{2,1,0:T(8,128)(2,1)S(1)} %bitcast.228), custom_call_target="tpu_custom_call" | custom-call | flops 4076863488 | bytes 12976128 | tf_op jit(solution)/shard_map/qkv_project/pallas_call | solution.py:238
  90.8 1.8 copy-done.6
  92.6 52.5 %attn_fwd.1 = (bf16[4,72,2048]{2,1,0:T(8,128)(2,1)S(1)}, f32[4,1,2048]{2,1,0:T(1,128)S(1)}, bf16[2,16,72,256]{3,2,1,0:T(8,128)(2,1)S(1)}, bf16[8,2,2,2,72,128]{5,4,3,2,1,0:T(8,128)(2,1)S(1)}) custom-call(bf16[4,3,72,2048]{3,2,1,0:T(8,128)(2,1)} %bitcast.232, bf16[2,2,2,72,128]{4,3,2,1,0:T(8,128)(2,1)S(1)} %bitcast.238), custom_call_target="tpu_custom_call" | custom-call | flops 4831838208 | bytes 4718592 | tf_op jit(solution)/shard_map/attn_fwd/pallas_call | solution.py:135
  146.1 1.1 copy-done.16
  147.2 6.3 %fusion.126 = (bf16[8,144,1152]{2,1,0:T(8,128)(2,1)}, bf16[8,144,1152]{2,1,0:T(8,128)(2,1)S(1)}, bf16[8,144,1152]{2,1,0:T(8,128)(2,1)S(1)}) fusion(bf16[8,432,1152]{2,1,0:T(8,128)(2,1)} %bitcast.243), kind=kLoop, calls=%fused_computation.195 | loop fusion | bytes 15925248 | tf_op jit(solution)/shard_map/slice | solution.py:455
  153.5 3.5 fusion.96
  158.0 1.9 fusion.76
  160.6 1.3 copy-done.14
  161.9 9.1 %cross_fwd.1 = (bf16[2,16,72,256]{3,2,1,0:T(8,128)(2,1)S(1)}, bf16[2,16,128,256]{3,2,1,0:T(8,128)(2,1)S(1)}) custom-call(s32[2]{0:T(128)S(1)} %copy-done.5, bf16[2,16,72,256]{3,2,1,0:T(8,128)(2,1)S(1)} %bitcast.219, bf16[8,2,2,2,72,128]{5,4,3,2,1,0:T(8,128)(2,1)S(1)} %copy-done.14), custom_call_target="tpu_custom_call" | custom-call | flops 2415919104 | bytes 4456448 | tf_op jit(solution)/shard_map/cross_fwd/pallas_call | solution.py:320
  171.1 2.2 convert_reduce_fusion
  174.3 1.5 fusion.81
  176.4 9.7 %reduce-scatter.5.cloned.1.call-start = ((), (), s32[]{:S(2)}) async-start(), calls=%async_computation.7 | async-start | bytes 1327104 | tf_op jit(solution)/shard_map/reduce_scatter | solution.py:363
  186.4 1.4 collective-permute-start
  187.9 11.0 %multiply_convert_fusion.1 = (bf16[2,256,2304]{2,1,0:T(8,128)(2,1)}, f32[2,256,2304]{2,1,0:T(8,128)}) fusion(f32[2304]{0:T(1024)S(1)} %convert_reduce_fusion.4, bf16[2,256,1152]{2,1,0:T(8,128)(2,1)} %fusion.81, bf16[2304,1152]{1,0:T(8,128)(2,1)} %all-gather.10.cloned.1.call-done), kind=kOutput, calls=%fused_computation.57 | convolution fusion | flops 2729705472 | bytes 13575168 | tf_op jit(solution)/shard_map/btd,fd->btf/dot_general | solution.py:24
  198.8 6.1 %collective-permute-done.1 = bf16[2,256,1152]{2,1,0:T(8,128)(2,1)} collective-permute-done((bf16[2,256,1152]{2,1,0:T(8,128)(2,1)}, bf16[2,256,1152]{2,1,0:T(8,128)(2,1)}, u32[]{:S(2)}, u32[]{:S(2)}) %collective-permute-start.1) | collective-permute-done | bytes 1179680 | tf_op jit(solution)/shard_map/ppermute | solution.py:367
  205.0 7.1 %multiply_convert_fusion = (bf16[2,256,2304]{2,1,0:T(8,128)(2,1)}, f32[2,256,2304]{2,1,0:T(8,128)}) fusion(f32[2304]{0:T(1024)S(1)} %convert_reduce_fusion.4, bf16[2,256,1152]{2,1,0:T(8,128)(2,1)} %collective-permute-done.1, bf16[2304,1152]{1,0:T(8,128)(2,1)S(1)} %copy-done.58), kind=kOutput, calls=%fused_computation.56 | convolution fusion | flops 2729705472 | bytes 13575168 | tf_op jit(solution)/shard_map/btd,fd->btf/dot_general | solution.py:24
  212.0 10.1 %all-gather.8.cloned.1.call-done = bf16[2304,1152]{1,0:T(8,128)(2,1)} async-done(((bf16[576,1152]{1,0:T(8,128)(2,1)}), bf16[2304,1152]{1,0:T(8,128)(2,1)}) %all-gather.8.cloned.1.call-update) | async-done | bytes 5308432 | tf_op jit(solution)/shard_map/all_gather | solution.py:359
  222.1 7.4 %collective-permute-done = bf16[2,256,1152]{2,1,0:T(8,128)(2,1)} collective-permute-done((bf16[2,256,1152]{2,1,0:T(8,128)(2,1)S(1)}, bf16[2,256,1152]{2,1,0:T(8,128)(2,1)}, u32[]{:S(2)}, u32[]{:S(2)}) %collective-permute-start) | collective-permute-done | bytes 1179680 | tf_op jit(solution)/shard_map/ppermute | solution.py:367
  229.5 9.0 %fusion = bf16[2304,1152]{1,0:T(8,128)(2,1)S(1)} fusion(bf16[2,256,2304]{2,1,0:T(8,128)(2,1)} %get-tuple-element.57, bf16[2,256,2304]{2,1,0:T(8,128)(2,1)} %get-tuple-element.56, bf16[2,256,1152]{2,1,0:T(8,128)(2,1)} %collective-permute-done, bf16[2,256,1152]{2,1,0:T(8,128)(2,1)S(1)} %copy-done.35), kind=kOutput, calls=%fused_computation.2 | convolution fusion | flops 5442011136 | bytes 12386304 | tf_op jit(solution)/shard_map/btf,btd->fd/dot_general | solution.py:24
  238.7 2.2 copy-done.59
  241.0 6.4 %fusion.128 = (f32[2304]{0:T(1024)S(1)}, bf16[2,256,2304]{2,1,0:T(8,128)(2,1)}) fusion(f32[2,256,2304]{2,1,0:T(8,128)S(1)} %copy-done.60, bf16[2,256,1152]{2,1,0:T(8,128)(2,1)S(1)} %copy-done.35, bf16[2304,1152]{1,0:T(8,128)(2,1)S(1)} %copy-done.59), kind=kOutput, calls=%fused_computation.197 | convolution fusion | flops 2742679296 | bytes 13575168 | tf_op jit(solution)/shard_map/btd,fd->btf/dot_general | solution.py:24
  247.4 7.9 %fusion.127 = (f32[2304]{0:T(1024)S(1)}, bf16[2,256,2304]{2,1,0:T(8,128)(2,1)}) fusion(f32[2,256,2304]{2,1,0:T(8,128)S(1)} %bitcast.274, bf16[2,256,1152]{2,1,0:T(8,128)(2,1)} %collective-permute-done, bf16[2304,1152]{1,0:T(8,128)(2,1)S(1)} %copy-done.59), kind=kOutput, calls=%fused_computation.196 | convolution fusion | flops 2742679296 | bytes 13575168 | tf_op jit(solution)/shard_map/btd,fd->btf/dot_general | solution.py:24
  255.3 9.1 %fusion.1 = bf16[2304,1152]{1,0:T(8,128)(2,1)S(1)} fusion(bf16[2,256,2304]{2,1,0:T(8,128)(2,1)} %get-tuple-element.117, bf16[2,256,2304]{2,1,0:T(8,128)(2,1)S(1)} %copy-done.62, bf16[2,256,1152]{2,1,0:T(8,128)(2,1)} %collective-permute-done.1, bf16[2,256,1152]{2,1,0:T(8,128)(2,1)} %fusion.81), kind=kOutput, calls=%fused_computation.3 | convolution fusion | flops 5442011136 | bytes 12386304 | tf_op jit(solution)/shard_map/btf,btd->fd/dot_general | solution.py:24
  264.7 5.0 fusion.56
  270.5 4.7 fusion.13
  275.1 5.9 %fusion.59 = bf16[2,256,1152]{2,1,0:T(8,128)(2,1)} fusion(bf16[2,256,2304]{2,1,0:T(8,128)(2,1)} %get-tuple-element.57, bf16[2304,1152]{1,0:T(8,128)(2,1)S(1)} %bitcast.267), kind=kOutput, calls=%fused_computation.75 | convolution fusion | flops 2718498816 | bytes 8847360 | tf_op jit(solution)/shard_map/btf,fd->btd/dot_general | solution.py:24
  281.1 2.2 fusion.8
  283.2 2.3 fusion.7
  285.5 13.1 %collective-permute-done.2 = bf16[2,256,1152]{2,1,0:T(8,128)(2,1)S(1)} collective-permute-done((bf16[2,256,1152]{2,1,0:T(8,128)(2,1)S(1)}, bf16[2,256,1152]{2,1,0:T(8,128)(2,1)S(1)}, u32[]{:S(2)}, u32[]{:S(2)}) %collective-permute-start.2) | collective-permute-done | bytes 1179680 | tf_op jit(solution)/shard_map/ppermute | solution.py:367
  298.6 3.9 fusion.85
  302.6 1.4 fusion.125
  303.9 1.4 copy-done.31
  305.3 2.7 convolution_convert_fusion.1
  308.1 1.3 copy-done.10
  309.3 1.6 copy-done.12
  310.9 1.3 copy-done.15
  312.2 9.3 %cross_bwd.1 = (bf16[2,16,72,256]{3,2,1,0:T(8,128)(2,1)S(1)}, bf16[8,2,2,2,72,128]{5,4,3,2,1,0:T(8,128)(2,1)}) custom-call(s32[2]{0:T(128)S(1)} %copy-done.5, bf16[2,16,72,256]{3,2,1,0:T(8,128)(2,1)S(1)} %bitcast.220, bf16[8,2,2,2,72,128]{5,4,3,2,1,0:T(8,128)(2,1)S(1)} %copy-done.15, bf16[2,16,128,256]{3,2,1,0:T(8,128)(2,1)S(1)} %copy-done.12, ...), custom_call_target="tpu_custom_call" | custom-call | flops 4831838208 | bytes 5636096 | tf_op jit(solution)/shard_map/cross_bwd/pallas_call | solution.py:348
  321.6 5.5 multiply_reduce_fusion.1
  327.1 1.4 copy-done.32
  328.5 3.3 fusion.6
  331.9 1.2 copy-done.38
  333.0 3.3 fusion.5
  337.9 4.9 fusion.4
  342.8 5.2 convolution_convert_fusion
  352.5 2.5 dynamic-slice_bitcast_fusion.3
  355.0 1.4 collective-permute-start.6
  356.4 2.5 dynamic-slice_bitcast_fusion.2
  359.5 140.4 %attn_bwd.1 = (bf16[4,3,72,2048]{3,2,1,0:T(8,128)(2,1)}, bf16[2,16,3,72,256]{4,3,2,1,0:T(8,128)(2,1)}, f32[8,16,1152]{2,1,0:T(8,128)}) custom-call(bf16[4,3,72,2048]{3,2,1,0:T(8,128)(2,1)} %bitcast.233, bf16[4,72,2048]{2,1,0:T(8,128)(2,1)} %copy-done.16, f32[4,1,2048]{2,1,0:T(1,128)} %copy-done.17, bf16[2,16,72,256]{3,2,1,0:T(8,128)(2,1)} %bitcast.272, ...), custom_call_target="tpu_custom_call" | custom-call | flops 12079595520 | bytes 11796480 | tf_op jit(solution)/shard_map/attn_bwd/pallas_call | solution.py:217
  500.0 1.3 reduce_sum.241
  503.4 4.2 fusion.97
  507.6 3.0 fusion.105
  510.7 2.7 fusion.77
  513.4 1.4 convolution_bitcast_fusion.6
  516.3 11.9 %fusion.94 = (f32[1152]{0:T(1024)S(1)}, f32[2,256]{1,0:T(2,128)S(1)}, f32[2,256]{1,0:T(2,128)S(1)}, f32[1152]{0:T(1024)S(1)}, f32[2,256,1152]{2,1,0:T(8,128)}) fusion(bf16[2,256,1152]{2,1,0:T(8,128)(2,1)S(1)} %copy-done.19, f32[2,256]{1,0:T(2,128)S(1)} %copy-done.52, f32[2,256]{1,0:T(2,128)S(1)} %copy-done.50, f32[2,1152]{1,0:T(2,128)S(1)} %copy-done.46, ...), kind=kOutput, calls=%fused_computation.116 | convolution fusion | flops 4082758656 | bytes 15067136 | tf_op jit(solution)/shard_map/bet,ed->btd/dot_general | solution.py:24
  528.3 17.0 %qkv_grad.1 = (bf16[432,1152]{1,0:T(8,128)(2,1)S(1)}, f32[432,1]{1,0:T(8,128)S(1)}, bf16[8,32,1152]{2,1,0:T(8,128)(2,1)S(1)}, f32[8,8,1152]{2,1,0:T(8,128)S(1)}) custom-call(bf16[2,432,2048]{2,1,0:T(8,128)(2,1)S(1)} %bitcast.234, bf16[8,544,1152]{2,1,0:T(8,128)(2,1)S(1)} %bitcast.231, bf16[8,32,1152]{2,1,0:T(8,128)(2,1)S(1)} %pad.18.parts, ...), custom_call_target="tpu_custom_call" | custom-call | flops 4076863488 | bytes 12976128 | tf_op jit(solution)/shard_map/qkv_grad/pallas_call | solution.py:281
  548.5 2.3 fusion.79
  550.7 4.2 fusion.93
  (264 shorter events, 30.1 us)
Async XLA Ops:
  7.2 70.5 %copy-start = (bf16[1152,2,144]{0,2,1:T(8,128)(2,1)S(1)}, bf16[1152,2,144]{0,2,1:T(8,128)(2,1)}, u32[]{:S(2)}) copy-start(bf16[1152,2,144]{0,2,1:T(8,128)(2,1)} %param.31) | copy-start | bytes 1990660
  7.2 5.7 %copy-start.18 = (bf16[2,256,1152]{2,1,0:T(8,128)(2,1)S(1)}, bf16[2,256,1152]{2,1,0:T(8,128)(2,1)}, u32[]{:S(2)}) copy-start(bf16[2,256,1152]{2,1,0:T(8,128)(2,1)} %param.20) | copy-start | bytes 3538948
  7.2 66.8 %all-gather.16.cloned.1.call-start = ((), (), s32[]{:S(2)}) async-start(), calls=%async_computation.12 | async-start | bytes 11280384 | tf_op jit(solution)/shard_map/all_gather | solution.py:359
  12.9 2.5 copy-start.49
  13.4 2.0 copy-start.51
  13.4 4.9 copy-start.47
  15.5 131.7 %all-gather.14.cloned.1.call-start = ((), (), s32[]{:S(2)}) async-start(), calls=%async_computation.11 | async-start | bytes 8957952 | tf_op jit(solution)/shard_map/all_gather | solution.py:359
  15.5 2.5 copy-start.53
  15.6 2.5 copy-start.54
  15.6 2.5 copy-start.56
  16.6 171.2 %all-gather.10.cloned.1.call-start = ((), (), s32[]{:S(2)}) async-start(), calls=%async_computation.5 | async-start | bytes 6635520 | tf_op jit(solution)/shard_map/all_gather | solution.py:359
  17.4 204.7 %all-gather.8.cloned.1.call-start = ((), (), s32[]{:S(2)}) async-start(), calls=%async_computation.4 | async-start | bytes 6635520 | tf_op jit(solution)/shard_map/all_gather | solution.py:359
  18.0 290.1 %all-gather.12.cloned.1.call-start = ((), (), s32[]{:S(2)}) async-start(), calls=%async_computation.6 | async-start | bytes 8957952 | tf_op jit(solution)/shard_map/all_gather | solution.py:359
  78.1 4.5 copy-start.4
  147.1 6.4 %copy-start.17 = (f32[4,1,2048]{2,1,0:T(1,128)}, f32[4,1,2048]{2,1,0:T(1,128)S(1)}, u32[]{:S(2)}) copy-start(f32[4,1,2048]{2,1,0:T(1,128)S(1)} %get-tuple-element.60.lse_ref) | copy-start | bytes 98308
  147.1 6.4 %copy-start.1 = (bf16[2,16,72,256]{3,2,1,0:T(8,128)(2,1)}, bf16[2,16,72,256]{3,2,1,0:T(8,128)(2,1)S(1)}, u32[]{:S(2)}) copy-start(bf16[2,16,72,256]{3,2,1,0:T(8,128)(2,1)S(1)} %get-tuple-element.49) | copy-start | bytes 3538948
  153.5 3.5 copy-start.30
  153.5 3.5 copy-start.29
  161.9 9.2 %copy-start.33 = (bf16[8,144,1152]{2,1,0:T(8,128)(2,1)S(1)}, bf16[8,144,1152]{2,1,0:T(8,128)(2,1)}, u32[]{:S(2)}) copy-start(bf16[8,144,1152]{2,1,0:T(8,128)(2,1)} %get-tuple-element.113) | copy-start | bytes 7962628
  161.9 9.2 %copy-start.37 = (bf16[2,256,1152]{2,1,0:T(8,128)(2,1)S(1)}, bf16[2,256,1152]{2,1,0:T(8,128)(2,1)}, u32[]{:S(2)}) copy-start(bf16[2,256,1152]{2,1,0:T(8,128)(2,1)} %copy-done.36) | copy-start | bytes 3538948
  171.0 2.2 copy-start.8
  171.0 2.2 copy-start.11
  173.3 13.1 %copy-start.35 = (bf16[2,256,1152]{2,1,0:T(8,128)(2,1)S(1)}, bf16[2,256,1152]{2,1,0:T(8,128)(2,1)}, u32[]{:S(2)}) copy-start(bf16[2,256,1152]{2,1,0:T(8,128)(2,1)} %get-tuple-element.54) | copy-start | bytes 3538948
  175.8 29.2 %collective-permute-start.1 = (bf16[2,256,1152]{2,1,0:T(8,128)(2,1)}, bf16[2,256,1152]{2,1,0:T(8,128)(2,1)}, u32[]{:S(2)}, u32[]{:S(2)}) collective-permute-start(bf16[2,256,1152]{2,1,0:T(8,128)(2,1)} %fusion.81), channel_id=1, source_target_pairs={{0,4},{4,0},{1,5},{5,1},{2,6},{6,2},{3,7},{7,3}} | collective-permute-start | bytes 3538952 | tf_op jit(solution)/shard_map/ppermute | solution.py:367
  176.4 337.0 %reduce-scatter.5.cloned.1.call-start = ((), (), s32[]{:S(2)}) async-start(), calls=%async_computation.7 | async-start | bytes 1327104 | tf_op jit(solution)/shard_map/reduce_scatter | solution.py:363
  186.4 43.1 %collective-permute-start = (bf16[2,256,1152]{2,1,0:T(8,128)(2,1)S(1)}, bf16[2,256,1152]{2,1,0:T(8,128)(2,1)}, u32[]{:S(2)}, u32[]{:S(2)}) collective-permute-start(bf16[2,256,1152]{2,1,0:T(8,128)(2,1)S(1)} %copy-done.35), channel_id=1, source_target_pairs={{0,4},{4,0},{1,5},{5,1},{2,6},{6,2},{3,7},{7,3}} | collective-permute-start | bytes 3538952 | tf_op jit(solution)/shard_map/ppermute | solution.py:367
  187.9 17.1 %copy-start.58 = (bf16[2304,1152]{1,0:T(8,128)(2,1)S(1)}, bf16[2304,1152]{1,0:T(8,128)(2,1)}, u32[]{:S(2)}) copy-start(bf16[2304,1152]{1,0:T(8,128)(2,1)} %all-gather.10.cloned.1.call-done) | copy-start | bytes 15925252
  229.5 9.2 %copy-start.60 = (f32[2,256,2304]{2,1,0:T(8,128)S(1)}, f32[2,256,2304]{2,1,0:T(8,128)}, u32[]{:S(2)}) copy-start(f32[2,256,2304]{2,1,0:T(8,128)} %get-tuple-element.135) | copy-start | bytes 14155780
  238.5 2.5 copy-start.59
  238.5 8.9 %slice-start.8 = ((s8[4718592]{0:T(1024)(128)(4,1)}), s8[4194304]{0:T(1024)(128)(4,1)S(1)}, s32[]{:S(2)}) async-start(s8[4718592]{0:T(1024)(128)(4,1)} %bitcast.273), calls=%async_computation.21 | async-start | bytes 8388608
  238.7 42.4 %collective-permute-start.3 = (bf16[2,576,1152]{2,1,0:T(8,128)(2,1)S(1)}, bf16[2,576,1152]{2,1,0:T(8,128)(2,1)S(1)}, u32[]{:S(2)}, u32[]{:S(2)}) collective-permute-start(bf16[2,576,1152]{2,1,0:T(8,128)(2,1)S(1)} %dynamic-slice_bitcast_fusion.1), channel_id=1, source_target_pairs={{0,1},{1,0},{2,3},{3,2},{4,5},{5,4},{6,7},{7,6}} | collective-permute-start | bytes 7962632 | tf_op jit(solution)/shard_map/ppermute | solution.py:367
  241.0 6.4 %slice-start.9 = ((s8[4718592]{0:T(1024)(128)(4,1)}), s8[524288]{0:T(1024)(128)(4,1)S(1)}, s32[]{:S(2)}) async-start(s8[4718592]{0:T(1024)(128)(4,1)} %bitcast.273), calls=%async_computation.22 | async-start | bytes 1048576
  247.4 7.9 %copy-start.62 = (bf16[2,256,2304]{2,1,0:T(8,128)(2,1)S(1)}, bf16[2,256,2304]{2,1,0:T(8,128)(2,1)}, u32[]{:S(2)}) copy-start(bf16[2,256,2304]{2,1,0:T(8,128)(2,1)} %get-tuple-element.119) | copy-start | bytes 7077892
  247.4 17.3 %slice-start.4 = ((s8[5308416]{0:T(1024)(128)(4,1)}), s8[4194304]{0:T(1024)(128)(4,1)S(1)}, s32[]{:S(2)}) async-start(s8[5308416]{0:T(1024)(128)(4,1)} %bitcast.264), calls=%async_computation.17 | async-start | bytes 8388608
  255.3 9.4 %slice-start.5 = ((s8[5308416]{0:T(1024)(128)(4,1)}), s8[1114112]{0:T(1024)(128)(4,1)S(1)}, s32[]{:S(2)}) async-start(s8[5308416]{0:T(1024)(128)(4,1)} %bitcast.264), calls=%async_computation.18 | async-start | bytes 2228224
  264.4 6.1 %slice-start.6 = ((s8[5308416]{0:T(1024)(128)(4,1)}), s8[1114112]{0:T(1024)(128)(4,1)S(1)}, s32[]{:S(2)}) async-start(s8[5308416]{0:T(1024)(128)(4,1)} %bitcast.266), calls=%async_computation.19 | async-start | bytes 2228224
  264.7 5.8 %slice-start.7 = ((s8[5308416]{0:T(1024)(128)(4,1)}), s8[4194304]{0:T(1024)(128)(4,1)S(1)}, s32[]{:S(2)}) async-start(s8[5308416]{0:T(1024)(128)(4,1)} %bitcast.266), calls=%async_computation.20 | async-start | bytes 8388608
  264.7 5.8 %copy-start.61 = (bf16[2,256,2304]{2,1,0:T(8,128)(2,1)S(1)}, bf16[2,256,2304]{2,1,0:T(8,128)(2,1)}, u32[]{:S(2)}) copy-start(bf16[2,256,2304]{2,1,0:T(8,128)(2,1)} %get-tuple-element.56) | copy-start | bytes 7077892
  264.7 18.5 %collective-permute-start.4 = (bf16[2,576,1152]{2,1,0:T(8,128)(2,1)S(1)}, bf16[2,576,1152]{2,1,0:T(8,128)(2,1)S(1)}, u32[]{:S(2)}, u32[]{:S(2)}) collective-permute-start(bf16[2,576,1152]{2,1,0:T(8,128)(2,1)S(1)} %dynamic-slice_bitcast_fusion), channel_id=1, source_target_pairs={{0,1},{1,0},{2,3},{3,2},{4,5},{5,4},{6,7},{7,6}} | collective-permute-start | bytes 7962632 | tf_op jit(solution)/shard_map/ppermute | solution.py:367
  269.8 28.8 %collective-permute-start.2 = (bf16[2,256,1152]{2,1,0:T(8,128)(2,1)S(1)}, bf16[2,256,1152]{2,1,0:T(8,128)(2,1)S(1)}, u32[]{:S(2)}, u32[]{:S(2)}) collective-permute-start(bf16[2,256,1152]{2,1,0:T(8,128)(2,1)S(1)} %fusion.56), channel_id=1, source_target_pairs={{0,4},{4,0},{1,5},{5,1},{2,6},{6,2},{3,7},{7,3}} | collective-permute-start | bytes 3538952 | tf_op jit(solution)/shard_map/ppermute | solution.py:367
  283.2 15.4 %copy-start.22 = (bf16[2,256,1152]{2,1,0:T(8,128)(2,1)S(1)}, bf16[2,256,1152]{2,1,0:T(8,128)(2,1)}, u32[]{:S(2)}) copy-start(bf16[2,256,1152]{2,1,0:T(8,128)(2,1)} %copy-done.21) | copy-start | bytes 3538948
  283.2 15.4 %copy-start.63 = (bf16[2,256,2304]{2,1,0:T(8,128)(2,1)S(1)}, bf16[2,256,2304]{2,1,0:T(8,128)(2,1)}, u32[]{:S(2)}) copy-start(bf16[2,256,2304]{2,1,0:T(8,128)(2,1)} %get-tuple-element.119) | copy-start | bytes 7077892
  285.5 17.0 %copy-start.25 = (bf16[2,256,1152]{2,1,0:T(8,128)(2,1)S(1)}, bf16[2,256,1152]{2,1,0:T(8,128)(2,1)}, u32[]{:S(2)}) copy-start(bf16[2,256,1152]{2,1,0:T(8,128)(2,1)} %param.39) | copy-start | bytes 3538948
  302.5 2.8 copy-start.34
  321.5 233.5 %reduce-scatter.7.cloned.1.call-start = ((), (), s32[]{:S(2)}) async-start(), calls=%async_computation.8 | async-start | bytes 2985984 | tf_op jit(solution)/shard_map/reduce_scatter | solution.py:363
  321.5 7.0 %copy-start.2 = (bf16[2,16,72,256]{3,2,1,0:T(8,128)(2,1)S(1)}, bf16[2,16,72,256]{3,2,1,0:T(8,128)(2,1)}, u32[]{:S(2)}) copy-start(bf16[2,16,72,256]{3,2,1,0:T(8,128)(2,1)} %copy-done.1) | copy-start | bytes 3538948
  331.8 223.2 %reduce-scatter.9.cloned.1.call-start = ((), (), s32[]{:S(2)}) async-start(), calls=%async_computation.9 | async-start | bytes 2985984 | tf_op jit(solution)/shard_map/reduce_scatter | solution.py:363
  336.4 218.6 %reduce-scatter.11.cloned.1.call-start = ((), (), s32[]{:S(2)}) async-start(), calls=%async_computation.10 | async-start | bytes 2985984 | tf_op jit(solution)/shard_map/reduce_scatter | solution.py:363
  352.0 151.3 %collective-permute-start.5 = (bf16[2,256,1152]{2,1,0:T(8,128)(2,1)}, bf16[2,256,1152]{2,1,0:T(8,128)(2,1)}, u32[]{:S(2)}, u32[]{:S(2)}) collective-permute-start(bf16[2,256,1152]{2,1,0:T(8,128)(2,1)} %fusion.59), channel_id=1, source_target_pairs={{0,4},{4,0},{1,5},{5,1},{2,6},{6,2},{3,7},{7,3}} | collective-permute-start | bytes 3538952 | tf_op jit(solution)/shard_map/ppermute | solution.py:367
  355.0 152.6 %collective-permute-start.6 = (bf16[576,1152]{1,0:T(8,128)(2,1)}, bf16[576,1152]{1,0:T(8,128)(2,1)}, u32[]{:S(2)}, u32[]{:S(2)}) collective-permute-start(bf16[576,1152]{1,0:T(8,128)(2,1)} %dynamic-slice_bitcast_fusion.3), channel_id=1, source_target_pairs={{0,2},{2,0},{1,3},{3,1},{4,6},{6,4},{5,7},{7,5}} | collective-permute-start | bytes 3981320 | tf_op jit(solution)/shard_map/ppermute | solution.py:367
  358.9 151.8 %collective-permute-start.7 = (bf16[576,1152]{1,0:T(8,128)(2,1)}, bf16[576,1152]{1,0:T(8,128)(2,1)}, u32[]{:S(2)}, u32[]{:S(2)}) collective-permute-start(bf16[576,1152]{1,0:T(8,128)(2,1)} %dynamic-slice_bitcast_fusion.2), channel_id=1, source_target_pairs={{0,2},{2,0},{1,3},{3,1},{4,6},{6,4},{5,7},{7,5}} | collective-permute-start | bytes 3981320 | tf_op jit(solution)/shard_map/ppermute | solution.py:367
  500.0 3.4 copy-start.23
  500.0 3.4 copy-start.26
  500.0 3.4 copy-start.48
  501.2 6.4 %copy-start.41 = (f32[16,1152]{1,0:T(8,128)}, f32[16,1152]{1,0:T(8,128)S(1)}, u32[]{:S(2)}) copy-start(f32[16,1152]{1,0:T(8,128)S(1)} %reduce_sum.241) | copy-start | bytes 221188
  503.4 4.3 copy-start.28
  507.6 3.1 copy-start.27
  514.8 13.5 %slice-start = ((s8[10027008]{0:T(1024)(128)(4,1)}), s8[4194304]{0:T(1024)(128)(4,1)S(1)}, s32[]{:S(2)}) async-start(s8[10027008]{0:T(1024)(128)(4,1)} %bitcast.229), calls=%async_computation.13 | async-start | bytes 8388608
  516.3 12.0 %slice-start.1 = ((s8[10027008]{0:T(1024)(128)(4,1)}), s8[4194304]{0:T(1024)(128)(4,1)S(1)}, s32[]{:S(2)}) async-start(s8[10027008]{0:T(1024)(128)(4,1)} %bitcast.229), calls=%async_computation.14 | async-start | bytes 8388608
  516.3 12.0 %slice-start.2 = ((s8[10027008]{0:T(1024)(128)(4,1)}), s8[1638400]{0:T(1024)(128)(4,1)S(1)}, s32[]{:S(2)}) async-start(s8[10027008]{0:T(1024)(128)(4,1)} %bitcast.229), calls=%async_computation.15 | async-start | bytes 3276800
  516.3 12.0 %copy-start.7 = (bf16[4,3,72,2048]{3,2,1,0:T(8,128)(2,1)S(1)}, bf16[4,3,72,2048]{3,2,1,0:T(8,128)(2,1)}, u32[]{:S(2)}) copy-start(bf16[4,3,72,2048]{3,2,1,0:T(8,128)(2,1)} %get-tuple-element.73) | copy-start | bytes 10616836
  528.3 17.1 %copy-start.39 = (bf16[1,2,2,2,72,128]{5,4,3,2,1,0:T(8,128)(2,1)S(1)}, bf16[1,2,2,2,72,128]{5,4,3,2,1,0:T(8,128)(2,1)}, u32[]{:S(2)}) copy-start(bf16[1,2,2,2,72,128]{5,4,3,2,1,0:T(8,128)(2,1)} %reduce-scatter.5.cloned.1.call-done) | copy-start | bytes 442372
  528.3 19.5 %slice-start.3 = ((f32[16,1152]{1,0:T(8,128)}), f32[3,1152]{1,0:T(4,128)S(1)}, s32[]{:S(2)}) async-start(f32[16,1152]{1,0:T(8,128)} %copy-done.41), calls=%async_computation.16 | async-start | bytes 36864 | tf_op jit(solution)/shard_map/slice | solution.py:539
  545.7 5.1 copy-start.20
  (27 other events, 36.5 us)
Sparse Core Ops, SparseCore 0:
  15.6 58.4 all-gather.15
  76.4 67.0 all-gather.13
  145.0 37.6 all-gather.9
  184.1 37.9 all-gather.7
  223.8 46.8 all-gather.11
  321.6 28.2 reduce-scatter.4
  353.9 45.6 reduce-scatter.6
  403.6 45.0 reduce-scatter.8
  502.1 38.6 reduce-scatter.10
where the time goes:
time: 573 us; the launch traced here: 563 us
  Pallas kernels  236 us (41%)
  matrix products  118 us (21%)
  waiting for transfers between devices  92.5 us (16%)
  local copies, waits for them, and re-layouts  51.7 us (9%)
  other arithmetic  33.1 us (6%)
  between operations  15.4 us (3%)
  starting transfers between devices  15.3 us (3%)
    pallas_call x1, Pallas kernels, attn_bwd(): pl.pallas_call(functools.partial(attn_bwd_kernel, hd ** (-0.5), blk, head...  140 us
    dot_general x23, matrix products, product(): return jnp.einsum(form, lhs, rhs, preferred_element_type=F32)  118 us
    all_gather x5, waiting for transfers between devices, gather_rows(): return lax.all_gather(tensor, axes, axis=0, tiled=True)  64.5 us
    pallas_call x1, Pallas kernels, attn_fwd(): pl.pallas_call(functools.partial(attn_fwd_kernel, hd ** (-0.5), blk, head...  52.5 us
    ppermute x8, waiting for transfers between devices, swap(): return lax.ppermute(tensor, axis, [(0, 1), (1, 0)])  26.7 us
    unnamed x153, local copies, waits for them, and re-layouts  26 us
    pallas_call x1, Pallas kernels, qkv_grad(): pl.pallas_call(qkv_grad_kernel, grid=(batch * N_DEV,), in_specs=[pl.Block...  17 us
  transfers between devices with their start and end apart: 17, of which 5 were waited for; matrix products, arithmetic and copies ran while one was open for 30% of the time, Pallas kernels for 40%

commit v1 on v0

--- a/solution.py
+++ b/solution.py
@@ -61,11 +61,14 @@
     return {'y': index // 4, 'x': (index // 2) % 2, 'c': index % 2}
 
 
-def entry_barrier(me):
+def barrier_signal(me):
     barrier = pltpu.get_barrier_semaphore()
     for k in range(1, N_DEV):
         pl.semaphore_signal(barrier, inc=1, device_id=device(me ^ k), device_id_type=pl.DeviceIdType.MESH)
-    pl.semaphore_wait(barrier, N_DEV - 1)
+
+
+def barrier_wait():
+    pl.semaphore_wait(pltpu.get_barrier_semaphore(), N_DEV - 1)
 
 
 def block_copy(src, dst, send_sem, recv_sem, peer, k):
@@ -102,8 +105,7 @@
 
     @pl.when(i == 0)
     def _():
-        entry_barrier(me)
-        start_all(kv_copies)
+        barrier_signal(me)
 
     def step(j, carry):
         cols = block_at(j, blk)
@@ -118,6 +120,12 @@
 
     lax.fori_loop(0, tokens // blk, step, 0, unroll=UNROLL)
     o_ref[0] = o_scr[i]
+
+    @pl.when(i == 0)
+    def _():
+        barrier_wait()
+        start_all(kv_copies)
+
     start_all(o_copies(i))
 
     @pl.when(i == last)
@@ -164,7 +172,8 @@
 
     @pl.when(i == 0)
     def _():
-        entry_barrier(me)
+        barrier_signal(me)
+        barrier_wait()
         for n in range(steps):
             start_all(g_copies(n))
         early_scr[...] = jnp.zeros_like(early_scr)
@@ -257,14 +266,18 @@
 
     @pl.when(n == 0)
     def _():
-        entry_barrier(me)
-        start_all(copies)
+        barrier_signal(me)
         w_acc[...] = jnp.zeros_like(w_acc)
         b_acc[...] = jnp.zeros_like(b_acc)
 
     g = g_ref[0]
     w_acc[...] += dot10(g, h_ref[0])
     b_acc[...] += g.astype(F32)
+
+    @pl.when(n == 0)
+    def _():
+        barrier_wait()
+        start_all(copies)
 
     @pl.when(n == pl.num_programs(0) - 1)
     def _():

time: 573 us -> 576 us (level)
  transfers between devices with their start and end apart: 17 -> 17, of which waited for: 5 -> 5; matrix products, arithmetic and copies ran while one was open for 30% -> 30% of each run, Pallas kernels for 40% -> 41%
where the time goes in v1:
time: 576 us; the launch traced here: 565 us
  Pallas kernels  239 us (41%)
  matrix products  118 us (20%)
  waiting for transfers between devices  92.6 us (16%)
  local copies, waits for them, and re-layouts  51.8 us (9%)
  other arithmetic  33 us (6%)
  between operations  15.4 us (3%)
  starting transfers between devices  15.3 us (3%)
    pallas_call x1, Pallas kernels, attn_bwd(): pl.pallas_call(functools.partial(attn_bwd_kernel, hd ** (-0.5), blk, head...  140 us
    dot_general x23, matrix products, product(): return jnp.einsum(form, lhs, rhs, preferred_element_type=F32)  118 us
    all_gather x5, waiting for transfers between devices, gather_rows(): return lax.all_gather(tensor, axes, axis=0, tiled=True)  65.3 us
    pallas_call x1, Pallas kernels, attn_fwd(): pl.pallas_call(functools.partial(attn_fwd_kernel, hd ** (-0.5), blk, head...  55.8 us
    ppermute x8, waiting for transfers between devices, swap(): return lax.ppermute(tensor, axis, [(0, 1), (1, 0)])  26 us
    unnamed x153, local copies, waits for them, and re-layouts  26 us
    pallas_call x1, Pallas kernels, qkv_grad(): pl.pallas_call(qkv_grad_kernel, grid=(batch * N_DEV,), in_specs=[pl.Block...  17.1 us
  transfers between devices with their start and end apart: 17, of which 5 were waited for; matrix products, arithmetic and copies ran while one was open for 30% of the time, Pallas kernels for 41%

profile of v1, /device:TPU:0, one launch (start us, length us, event | category | flops | bytes accessed | tf_op | source)
XLA Modules:
  0.0 565.4 jit_solution(10672444224613955593)
XLA Ops:
  11.4 1.5 convert_reduce_fusion.1
  14.1 1.3 maximum_maximum_fusion
  15.6 1.0 pad_maximum_fusion
  18.3 1.3 fusion.68
  19.6 54.4 %all-gather.16.cloned.1.call-done = bf16[4352,1152]{1,0:T(8,128)(2,1)} async-done(((bf16[544,1152]{1,0:T(8,128)(2,1)}), bf16[4352,1152]{1,0:T(8,128)(2,1)}) %all-gather.16.cloned.1.call-update) | async-done | bytes 10027024 | tf_op jit(solution)/shard_map/all_gather | solution.py:372
  75.0 1.1 slice.100
  78.1 4.5 copy-done.4
  82.6 8.2 %qkv_project.1 = bf16[2,432,2048]{2,1,0:T(8,128)(2,1)S(1)} custom-call(bf16[432,1152]{1,0:T(8,128)(2,1)S(1)} %bitcast.225, f32[432,1]{1,0:T(8,128)S(1)} %reshape.312.b_ref, bf16[8,544,1152]{2,1,0:T(8,128)(2,1)S(1)} %bitcast.228), custom_call_target="tpu_custom_call" | custom-call | flops 4076863488 | bytes 12976128 | tf_op jit(solution)/shard_map/qkv_project/pallas_call | solution.py:247
  90.8 1.8 copy-done.6
  92.6 55.8 %attn_fwd.1 = (bf16[4,72,2048]{2,1,0:T(8,128)(2,1)S(1)}, f32[4,1,2048]{2,1,0:T(1,128)S(1)}, bf16[2,16,72,256]{3,2,1,0:T(8,128)(2,1)S(1)}, bf16[8,2,2,2,72,128]{5,4,3,2,1,0:T(8,128)(2,1)S(1)}) custom-call(bf16[4,3,72,2048]{3,2,1,0:T(8,128)(2,1)} %bitcast.232, bf16[2,2,2,72,128]{4,3,2,1,0:T(8,128)(2,1)S(1)} %bitcast.238), custom_call_target="tpu_custom_call" | custom-call | flops 4831838208 | bytes 4718592 | tf_op jit(solution)/shard_map/attn_fwd/pallas_call | solution.py:143
  149.4 1.1 copy-done.16
  150.6 6.3 %fusion.126 = (bf16[8,144,1152]{2,1,0:T(8,128)(2,1)}, bf16[8,144,1152]{2,1,0:T(8,128)(2,1)S(1)}, bf16[8,144,1152]{2,1,0:T(8,128)(2,1)S(1)}) fusion(bf16[8,432,1152]{2,1,0:T(8,128)(2,1)} %bitcast.243), kind=kLoop, calls=%fused_computation.195 | loop fusion | bytes 15925248 | tf_op jit(solution)/shard_map/slice | solution.py:468
  156.9 3.5 fusion.96
  161.4 1.9 fusion.76
  163.9 1.3 copy-done.14
  165.2 9.1 %cross_fwd.1 = (bf16[2,16,72,256]{3,2,1,0:T(8,128)(2,1)S(1)}, bf16[2,16,128,256]{3,2,1,0:T(8,128)(2,1)S(1)}) custom-call(s32[2]{0:T(128)S(1)} %copy-done.5, bf16[2,16,72,256]{3,2,1,0:T(8,128)(2,1)S(1)} %bitcast.219, bf16[8,2,2,2,72,128]{5,4,3,2,1,0:T(8,128)(2,1)S(1)} %copy-done.14), custom_call_target="tpu_custom_call" | custom-call | flops 2415919104 | bytes 4456448 | tf_op jit(solution)/shard_map/cross_fwd/pallas_call | solution.py:333
  174.4 2.2 convert_reduce_fusion
  177.6 1.5 fusion.81
  179.3 9.7 %reduce-scatter.5.cloned.1.call-start = ((), (), s32[]{:S(2)}) async-start(), calls=%async_computation.7 | async-start | bytes 1327104 | tf_op jit(solution)/shard_map/reduce_scatter | solution.py:376
  189.2 1.9 collective-permute-start
  191.2 10.7 %multiply_convert_fusion.1 = (bf16[2,256,2304]{2,1,0:T(8,128)(2,1)}, f32[2,256,2304]{2,1,0:T(8,128)}) fusion(f32[2304]{0:T(1024)S(1)} %convert_reduce_fusion.4, bf16[2,256,1152]{2,1,0:T(8,128)(2,1)} %fusion.81, bf16[2304,1152]{1,0:T(8,128)(2,1)} %all-gather.10.cloned.1.call-done), kind=kOutput, calls=%fused_computation.57 | convolution fusion | flops 2729705472 | bytes 13575168 | tf_op jit(solution)/shard_map/btd,fd->btf/dot_general | solution.py:24
  201.9 6.4 %collective-permute-done.1 = bf16[2,256,1152]{2,1,0:T(8,128)(2,1)} collective-permute-done((bf16[2,256,1152]{2,1,0:T(8,128)(2,1)}, bf16[2,256,1152]{2,1,0:T(8,128)(2,1)}, u32[]{:S(2)}, u32[]{:S(2)}) %collective-permute-start.1) | collective-permute-done | bytes 1179680 | tf_op jit(solution)/shard_map/ppermute | solution.py:380
  208.3 7.1 %multiply_convert_fusion = (bf16[2,256,2304]{2,1,0:T(8,128)(2,1)}, f32[2,256,2304]{2,1,0:T(8,128)}) fusion(f32[2304]{0:T(1024)S(1)} %convert_reduce_fusion.4, bf16[2,256,1152]{2,1,0:T(8,128)(2,1)} %collective-permute-done.1, bf16[2304,1152]{1,0:T(8,128)(2,1)S(1)} %copy-done.58), kind=kOutput, calls=%fused_computation.56 | convolution fusion | flops 2729705472 | bytes 13575168 | tf_op jit(solution)/shard_map/btd,fd->btf/dot_general | solution.py:24
  215.4 10.9 %all-gather.8.cloned.1.call-done = bf16[2304,1152]{1,0:T(8,128)(2,1)} async-done(((bf16[576,1152]{1,0:T(8,128)(2,1)}), bf16[2304,1152]{1,0:T(8,128)(2,1)}) %all-gather.8.cloned.1.call-update) | async-done | bytes 5308432 | tf_op jit(solution)/shard_map/all_gather | solution.py:372
  226.2 6.5 %collective-permute-done = bf16[2,256,1152]{2,1,0:T(8,128)(2,1)} collective-permute-done((bf16[2,256,1152]{2,1,0:T(8,128)(2,1)S(1)}, bf16[2,256,1152]{2,1,0:T(8,128)(2,1)}, u32[]{:S(2)}, u32[]{:S(2)}) %collective-permute-start) | collective-permute-done | bytes 1179680 | tf_op jit(solution)/shard_map/ppermute | solution.py:380
  232.8 9.1 %fusion = bf16[2304,1152]{1,0:T(8,128)(2,1)S(1)} fusion(bf16[2,256,2304]{2,1,0:T(8,128)(2,1)} %get-tuple-element.57, bf16[2,256,2304]{2,1,0:T(8,128)(2,1)} %get-tuple-element.56, bf16[2,256,1152]{2,1,0:T(8,128)(2,1)} %collective-permute-done, bf16[2,256,1152]{2,1,0:T(8,128)(2,1)S(1)} %copy-done.35), kind=kOutput, calls=%fused_computation.2 | convolution fusion | flops 5442011136 | bytes 12386304 | tf_op jit(solution)/shard_map/btf,btd->fd/dot_general | solution.py:24
  242.2 2.2 copy-done.59
  244.4 6.5 %fusion.128 = (f32[2304]{0:T(1024)S(1)}, bf16[2,256,2304]{2,1,0:T(8,128)(2,1)}) fusion(f32[2,256,2304]{2,1,0:T(8,128)S(1)} %copy-done.60, bf16[2,256,1152]{2,1,0:T(8,128)(2,1)S(1)} %copy-done.35, bf16[2304,1152]{1,0:T(8,128)(2,1)S(1)} %copy-done.59), kind=kOutput, calls=%fused_computation.197 | convolution fusion | flops 2742679296 | bytes 13575168 | tf_op jit(solution)/shard_map/btd,fd->btf/dot_general | solution.py:24
  250.9 7.9 %fusion.127 = (f32[2304]{0:T(1024)S(1)}, bf16[2,256,2304]{2,1,0:T(8,128)(2,1)}) fusion(f32[2,256,2304]{2,1,0:T(8,128)S(1)} %bitcast.274, bf16[2,256,1152]{2,1,0:T(8,128)(2,1)} %collective-permute-done, bf16[2304,1152]{1,0:T(8,128)(2,1)S(1)} %copy-done.59), kind=kOutput, calls=%fused_computation.196 | convolution fusion | flops 2742679296 | bytes 13575168 | tf_op jit(solution)/shard_map/btd,fd->btf/dot_general | solution.py:24
  258.8 9.0 %fusion.1 = bf16[2304,1152]{1,0:T(8,128)(2,1)S(1)} fusion(bf16[2,256,2304]{2,1,0:T(8,128)(2,1)} %get-tuple-element.117, bf16[2,256,2304]{2,1,0:T(8,128)(2,1)S(1)} %copy-done.62, bf16[2,256,1152]{2,1,0:T(8,128)(2,1)} %collective-permute-done.1, bf16[2,256,1152]{2,1,0:T(8,128)(2,1)} %fusion.81), kind=kOutput, calls=%fused_computation.3 | convolution fusion | flops 5442011136 | bytes 12386304 | tf_op jit(solution)/shard_map/btf,btd->fd/dot_general | solution.py:24
  268.1 5.2 fusion.56
  274.0 4.7 fusion.13
  278.6 5.9 %fusion.59 = bf16[2,256,1152]{2,1,0:T(8,128)(2,1)} fusion(bf16[2,256,2304]{2,1,0:T(8,128)(2,1)} %get-tuple-element.57, bf16[2304,1152]{1,0:T(8,128)(2,1)S(1)} %bitcast.267), kind=kOutput, calls=%fused_computation.75 | convolution fusion | flops 2718498816 | bytes 8847360 | tf_op jit(solution)/shard_map/btf,fd->btd/dot_general | solution.py:24
  284.5 2.2 fusion.8
  286.7 2.3 fusion.7
  289.0 13.0 %collective-permute-done.2 = bf16[2,256,1152]{2,1,0:T(8,128)(2,1)S(1)} collective-permute-done((bf16[2,256,1152]{2,1,0:T(8,128)(2,1)S(1)}, bf16[2,256,1152]{2,1,0:T(8,128)(2,1)S(1)}, u32[]{:S(2)}, u32[]{:S(2)}) %collective-permute-start.2) | collective-permute-done | bytes 1179680 | tf_op jit(solution)/shard_map/ppermute | solution.py:380
  302.0 3.9 fusion.85
  306.0 1.4 fusion.125
  307.3 1.4 copy-done.31
  308.7 2.7 convolution_convert_fusion.1
  311.5 1.3 copy-done.10
  312.7 1.6 copy-done.12
  314.3 1.3 copy-done.15
  315.6 9.3 %cross_bwd.1 = (bf16[2,16,72,256]{3,2,1,0:T(8,128)(2,1)S(1)}, bf16[8,2,2,2,72,128]{5,4,3,2,1,0:T(8,128)(2,1)}) custom-call(s32[2]{0:T(128)S(1)} %copy-done.5, bf16[2,16,72,256]{3,2,1,0:T(8,128)(2,1)S(1)} %bitcast.220, bf16[8,2,2,2,72,128]{5,4,3,2,1,0:T(8,128)(2,1)S(1)} %copy-done.15, bf16[2,16,128,256]{3,2,1,0:T(8,128)(2,1)S(1)} %copy-done.12, ...), custom_call_target="tpu_custom_call" | custom-call | flops 4831838208 | bytes 5636096 | tf_op jit(solution)/shard_map/cross_bwd/pallas_call | solution.py:361
  324.9 5.5 multiply_reduce_fusion.1
  330.5 1.4 copy-done.32
  331.9 3.3 fusion.6
  335.2 1.2 copy-done.38
  336.4 3.3 fusion.5
  341.3 4.9 fusion.4
  346.2 5.3 convolution_convert_fusion
  356.0 2.5 dynamic-slice_bitcast_fusion.3
  358.5 2.5 dynamic-slice_bitcast_fusion.2
  361.0 2.0 collective-permute-start.7
  363.1 139.6 %attn_bwd.1 = (bf16[4,3,72,2048]{3,2,1,0:T(8,128)(2,1)}, bf16[2,16,3,72,256]{4,3,2,1,0:T(8,128)(2,1)}, f32[8,16,1152]{2,1,0:T(8,128)}) custom-call(bf16[4,3,72,2048]{3,2,1,0:T(8,128)(2,1)} %bitcast.233, bf16[4,72,2048]{2,1,0:T(8,128)(2,1)} %copy-done.16, f32[4,1,2048]{2,1,0:T(1,128)} %copy-done.17, bf16[2,16,72,256]{3,2,1,0:T(8,128)(2,1)} %bitcast.272, ...), custom_call_target="tpu_custom_call" | custom-call | flops 12079595520 | bytes 11796480 | tf_op jit(solution)/shard_map/attn_bwd/pallas_call | solution.py:226
  502.7 1.3 reduce_sum.241
  506.0 4.0 fusion.97
  510.1 3.0 fusion.105
  513.1 2.8 fusion.77
  515.9 1.4 convolution_bitcast_fusion.6
  518.9 11.9 %fusion.94 = (f32[1152]{0:T(1024)S(1)}, f32[2,256]{1,0:T(2,128)S(1)}, f32[2,256]{1,0:T(2,128)S(1)}, f32[1152]{0:T(1024)S(1)}, f32[2,256,1152]{2,1,0:T(8,128)}) fusion(bf16[2,256,1152]{2,1,0:T(8,128)(2,1)S(1)} %copy-done.19, f32[2,256]{1,0:T(2,128)S(1)} %copy-done.52, f32[2,256]{1,0:T(2,128)S(1)} %copy-done.50, f32[2,1152]{1,0:T(2,128)S(1)} %copy-done.46, ...), kind=kOutput, calls=%fused_computation.116 | convolution fusion | flops 4082758656 | bytes 15067136 | tf_op jit(solution)/shard_map/bet,ed->btd/dot_general | solution.py:24
  530.9 17.1 %qkv_grad.1 = (bf16[432,1152]{1,0:T(8,128)(2,1)S(1)}, f32[432,1]{1,0:T(8,128)S(1)}, bf16[8,32,1152]{2,1,0:T(8,128)(2,1)S(1)}, f32[8,8,1152]{2,1,0:T(8,128)S(1)}) custom-call(bf16[2,432,2048]{2,1,0:T(8,128)(2,1)S(1)} %bitcast.234, bf16[8,544,1152]{2,1,0:T(8,128)(2,1)S(1)} %bitcast.231, bf16[8,32,1152]{2,1,0:T(8,128)(2,1)S(1)} %pad.18.parts, ...), custom_call_target="tpu_custom_call" | custom-call | flops 4076863488 | bytes 12976128 | tf_op jit(solution)/shard_map/qkv_grad/pallas_call | solution.py:294
  551.1 2.2 fusion.79
  553.3 4.2 fusion.93
  (264 shorter events, 28.9 us)
Async XLA Ops:
  7.2 70.5 %copy-start = (bf16[1152,2,144]{0,2,1:T(8,128)(2,1)S(1)}, bf16[1152,2,144]{0,2,1:T(8,128)(2,1)}, u32[]{:S(2)}) copy-start(bf16[1152,2,144]{0,2,1:T(8,128)(2,1)} %param.31) | copy-start | bytes 1990660
  7.2 5.7 %copy-start.18 = (bf16[2,256,1152]{2,1,0:T(8,128)(2,1)S(1)}, bf16[2,256,1152]{2,1,0:T(8,128)(2,1)}, u32[]{:S(2)}) copy-start(bf16[2,256,1152]{2,1,0:T(8,128)(2,1)} %param.20) | copy-start | bytes 3538948
  7.2 66.8 %all-gather.16.cloned.1.call-start = ((), (), s32[]{:S(2)}) async-start(), calls=%async_computation.12 | async-start | bytes 11280384 | tf_op jit(solution)/shard_map/all_gather | solution.py:372
  12.9 2.5 copy-start.49
  13.4 2.0 copy-start.51
  13.4 4.9 copy-start.47
  15.5 135.0 %all-gather.14.cloned.1.call-start = ((), (), s32[]{:S(2)}) async-start(), calls=%async_computation.11 | async-start | bytes 8957952 | tf_op jit(solution)/shard_map/all_gather | solution.py:372
  15.5 2.5 copy-start.53
  15.6 2.5 copy-start.54
  15.6 2.5 copy-start.56
  16.6 174.5 %all-gather.10.cloned.1.call-start = ((), (), s32[]{:S(2)}) async-start(), calls=%async_computation.5 | async-start | bytes 6635520 | tf_op jit(solution)/shard_map/all_gather | solution.py:372
  17.4 208.9 %all-gather.8.cloned.1.call-start = ((), (), s32[]{:S(2)}) async-start(), calls=%async_computation.4 | async-start | bytes 6635520 | tf_op jit(solution)/shard_map/all_gather | solution.py:372
  18.0 293.5 %all-gather.12.cloned.1.call-start = ((), (), s32[]{:S(2)}) async-start(), calls=%async_computation.6 | async-start | bytes 8957952 | tf_op jit(solution)/shard_map/all_gather | solution.py:372
  78.1 4.5 copy-start.4
  150.5 6.4 %copy-start.17 = (f32[4,1,2048]{2,1,0:T(1,128)}, f32[4,1,2048]{2,1,0:T(1,128)S(1)}, u32[]{:S(2)}) copy-start(f32[4,1,2048]{2,1,0:T(1,128)S(1)} %get-tuple-element.60.lse_ref) | copy-start | bytes 98308
  150.5 6.4 %copy-start.1 = (bf16[2,16,72,256]{3,2,1,0:T(8,128)(2,1)}, bf16[2,16,72,256]{3,2,1,0:T(8,128)(2,1)S(1)}, u32[]{:S(2)}) copy-start(bf16[2,16,72,256]{3,2,1,0:T(8,128)(2,1)S(1)} %get-tuple-element.49) | copy-start | bytes 3538948
  156.9 3.5 copy-start.30
  156.9 3.5 copy-start.29
  165.2 9.2 %copy-start.33 = (bf16[8,144,1152]{2,1,0:T(8,128)(2,1)S(1)}, bf16[8,144,1152]{2,1,0:T(8,128)(2,1)}, u32[]{:S(2)}) copy-start(bf16[8,144,1152]{2,1,0:T(8,128)(2,1)} %get-tuple-element.113) | copy-start | bytes 7962628
  165.2 9.2 %copy-start.37 = (bf16[2,256,1152]{2,1,0:T(8,128)(2,1)S(1)}, bf16[2,256,1152]{2,1,0:T(8,128)(2,1)}, u32[]{:S(2)}) copy-start(bf16[2,256,1152]{2,1,0:T(8,128)(2,1)} %copy-done.36) | copy-start | bytes 3538948
  174.4 2.2 copy-start.8
  174.4 2.2 copy-start.11
  176.6 12.6 %copy-start.35 = (bf16[2,256,1152]{2,1,0:T(8,128)(2,1)S(1)}, bf16[2,256,1152]{2,1,0:T(8,128)(2,1)}, u32[]{:S(2)}) copy-start(bf16[2,256,1152]{2,1,0:T(8,128)(2,1)} %get-tuple-element.54) | copy-start | bytes 3538948
  179.1 29.2 %collective-permute-start.1 = (bf16[2,256,1152]{2,1,0:T(8,128)(2,1)}, bf16[2,256,1152]{2,1,0:T(8,128)(2,1)}, u32[]{:S(2)}, u32[]{:S(2)}) collective-permute-start(bf16[2,256,1152]{2,1,0:T(8,128)(2,1)} %fusion.81), channel_id=1, source_target_pairs={{0,4},{4,0},{1,5},{5,1},{2,6},{6,2},{3,7},{7,3}} | collective-permute-start | bytes 3538952 | tf_op jit(solution)/shard_map/ppermute | solution.py:380
  179.3 336.6 %reduce-scatter.5.cloned.1.call-start = ((), (), s32[]{:S(2)}) async-start(), calls=%async_computation.7 | async-start | bytes 1327104 | tf_op jit(solution)/shard_map/reduce_scatter | solution.py:376
  189.2 43.5 %collective-permute-start = (bf16[2,256,1152]{2,1,0:T(8,128)(2,1)S(1)}, bf16[2,256,1152]{2,1,0:T(8,128)(2,1)}, u32[]{:S(2)}, u32[]{:S(2)}) collective-permute-start(bf16[2,256,1152]{2,1,0:T(8,128)(2,1)S(1)} %copy-done.35), channel_id=1, source_target_pairs={{0,4},{4,0},{1,5},{5,1},{2,6},{6,2},{3,7},{7,3}} | collective-permute-start | bytes 3538952 | tf_op jit(solution)/shard_map/ppermute | solution.py:380
  191.2 17.1 %copy-start.58 = (bf16[2304,1152]{1,0:T(8,128)(2,1)S(1)}, bf16[2304,1152]{1,0:T(8,128)(2,1)}, u32[]{:S(2)}) copy-start(bf16[2304,1152]{1,0:T(8,128)(2,1)} %all-gather.10.cloned.1.call-done) | copy-start | bytes 15925252
  232.8 9.4 %copy-start.60 = (f32[2,256,2304]{2,1,0:T(8,128)S(1)}, f32[2,256,2304]{2,1,0:T(8,128)}, u32[]{:S(2)}) copy-start(f32[2,256,2304]{2,1,0:T(8,128)} %get-tuple-element.135) | copy-start | bytes 14155780
  241.9 2.5 copy-start.59
  241.9 9.0 %slice-start.8 = ((s8[4718592]{0:T(1024)(128)(4,1)}), s8[4194304]{0:T(1024)(128)(4,1)S(1)}, s32[]{:S(2)}) async-start(s8[4718592]{0:T(1024)(128)(4,1)} %bitcast.273), calls=%async_computation.21 | async-start | bytes 8388608
  242.1 42.4 %collective-permute-start.3 = (bf16[2,576,1152]{2,1,0:T(8,128)(2,1)S(1)}, bf16[2,576,1152]{2,1,0:T(8,128)(2,1)S(1)}, u32[]{:S(2)}, u32[]{:S(2)}) collective-permute-start(bf16[2,576,1152]{2,1,0:T(8,128)(2,1)S(1)} %dynamic-slice_bitcast_fusion.1), channel_id=1, source_target_pairs={{0,1},{1,0},{2,3},{3,2},{4,5},{5,4},{6,7},{7,6}} | collective-permute-start | bytes 7962632 | tf_op jit(solution)/shard_map/ppermute | solution.py:380
  244.4 6.5 %slice-start.9 = ((s8[4718592]{0:T(1024)(128)(4,1)}), s8[524288]{0:T(1024)(128)(4,1)S(1)}, s32[]{:S(2)}) async-start(s8[4718592]{0:T(1024)(128)(4,1)} %bitcast.273), calls=%async_computation.22 | async-start | bytes 1048576
  250.8 7.9 %copy-start.62 = (bf16[2,256,2304]{2,1,0:T(8,128)(2,1)S(1)}, bf16[2,256,2304]{2,1,0:T(8,128)(2,1)}, u32[]{:S(2)}) copy-start(bf16[2,256,2304]{2,1,0:T(8,128)(2,1)} %get-tuple-element.119) | copy-start | bytes 7077892
  250.8 17.3 %slice-start.4 = ((s8[5308416]{0:T(1024)(128)(4,1)}), s8[4194304]{0:T(1024)(128)(4,1)S(1)}, s32[]{:S(2)}) async-start(s8[5308416]{0:T(1024)(128)(4,1)} %bitcast.264), calls=%async_computation.17 | async-start | bytes 8388608
  258.8 9.4 %slice-start.5 = ((s8[5308416]{0:T(1024)(128)(4,1)}), s8[1114112]{0:T(1024)(128)(4,1)S(1)}, s32[]{:S(2)}) async-start(s8[5308416]{0:T(1024)(128)(4,1)} %bitcast.264), calls=%async_computation.18 | async-start | bytes 2228224
  267.8 6.1 %slice-start.6 = ((s8[5308416]{0:T(1024)(128)(4,1)}), s8[1114112]{0:T(1024)(128)(4,1)S(1)}, s32[]{:S(2)}) async-start(s8[5308416]{0:T(1024)(128)(4,1)} %bitcast.266), calls=%async_computation.19 | async-start | bytes 2228224
  268.1 5.9 %slice-start.7 = ((s8[5308416]{0:T(1024)(128)(4,1)}), s8[4194304]{0:T(1024)(128)(4,1)S(1)}, s32[]{:S(2)}) async-start(s8[5308416]{0:T(1024)(128)(4,1)} %bitcast.266), calls=%async_computation.20 | async-start | bytes 8388608
  268.1 5.9 %copy-start.61 = (bf16[2,256,2304]{2,1,0:T(8,128)(2,1)S(1)}, bf16[2,256,2304]{2,1,0:T(8,128)(2,1)}, u32[]{:S(2)}) copy-start(bf16[2,256,2304]{2,1,0:T(8,128)(2,1)} %get-tuple-element.56) | copy-start | bytes 7077892
  268.1 18.6 %collective-permute-start.4 = (bf16[2,576,1152]{2,1,0:T(8,128)(2,1)S(1)}, bf16[2,576,1152]{2,1,0:T(8,128)(2,1)S(1)}, u32[]{:S(2)}, u32[]{:S(2)}) collective-permute-start(bf16[2,576,1152]{2,1,0:T(8,128)(2,1)S(1)} %dynamic-slice_bitcast_fusion), channel_id=1, source_target_pairs={{0,1},{1,0},{2,3},{3,2},{4,5},{5,4},{6,7},{7,6}} | collective-permute-start | bytes 7962632 | tf_op jit(solution)/shard_map/ppermute | solution.py:380
  273.3 28.7 %collective-permute-start.2 = (bf16[2,256,1152]{2,1,0:T(8,128)(2,1)S(1)}, bf16[2,256,1152]{2,1,0:T(8,128)(2,1)S(1)}, u32[]{:S(2)}, u32[]{:S(2)}) collective-permute-start(bf16[2,256,1152]{2,1,0:T(8,128)(2,1)S(1)} %fusion.56), channel_id=1, source_target_pairs={{0,4},{4,0},{1,5},{5,1},{2,6},{6,2},{3,7},{7,3}} | collective-permute-start | bytes 3538952 | tf_op jit(solution)/shard_map/ppermute | solution.py:380
  286.7 15.3 %copy-start.22 = (bf16[2,256,1152]{2,1,0:T(8,128)(2,1)S(1)}, bf16[2,256,1152]{2,1,0:T(8,128)(2,1)}, u32[]{:S(2)}) copy-start(bf16[2,256,1152]{2,1,0:T(8,128)(2,1)} %copy-done.21) | copy-start | bytes 3538948
  286.7 15.3 %copy-start.63 = (bf16[2,256,2304]{2,1,0:T(8,128)(2,1)S(1)}, bf16[2,256,2304]{2,1,0:T(8,128)(2,1)}, u32[]{:S(2)}) copy-start(bf16[2,256,2304]{2,1,0:T(8,128)(2,1)} %get-tuple-element.119) | copy-start | bytes 7077892
  289.0 16.9 %copy-start.25 = (bf16[2,256,1152]{2,1,0:T(8,128)(2,1)S(1)}, bf16[2,256,1152]{2,1,0:T(8,128)(2,1)}, u32[]{:S(2)}) copy-start(bf16[2,256,1152]{2,1,0:T(8,128)(2,1)} %param.39) | copy-start | bytes 3538948
  305.9 2.8 copy-start.34
  324.9 232.7 %reduce-scatter.7.cloned.1.call-start = ((), (), s32[]{:S(2)}) async-start(), calls=%async_computation.8 | async-start | bytes 2985984 | tf_op jit(solution)/shard_map/reduce_scatter | solution.py:376
  324.9 7.0 %copy-start.2 = (bf16[2,16,72,256]{3,2,1,0:T(8,128)(2,1)S(1)}, bf16[2,16,72,256]{3,2,1,0:T(8,128)(2,1)}, u32[]{:S(2)}) copy-start(bf16[2,16,72,256]{3,2,1,0:T(8,128)(2,1)} %copy-done.1) | copy-start | bytes 3538948
  335.2 222.4 %reduce-scatter.9.cloned.1.call-start = ((), (), s32[]{:S(2)}) async-start(), calls=%async_computation.9 | async-start | bytes 2985984 | tf_op jit(solution)/shard_map/reduce_scatter | solution.py:376
  339.8 217.8 %reduce-scatter.11.cloned.1.call-start = ((), (), s32[]{:S(2)}) async-start(), calls=%async_computation.10 | async-start | bytes 2985984 | tf_op jit(solution)/shard_map/reduce_scatter | solution.py:376
  355.5 150.5 %collective-permute-start.5 = (bf16[2,256,1152]{2,1,0:T(8,128)(2,1)}, bf16[2,256,1152]{2,1,0:T(8,128)(2,1)}, u32[]{:S(2)}, u32[]{:S(2)}) collective-permute-start(bf16[2,256,1152]{2,1,0:T(8,128)(2,1)} %fusion.59), channel_id=1, source_target_pairs={{0,4},{4,0},{1,5},{5,1},{2,6},{6,2},{3,7},{7,3}} | collective-permute-start | bytes 3538952 | tf_op jit(solution)/shard_map/ppermute | solution.py:380
  358.5 151.6 %collective-permute-start.6 = (bf16[576,1152]{1,0:T(8,128)(2,1)}, bf16[576,1152]{1,0:T(8,128)(2,1)}, u32[]{:S(2)}, u32[]{:S(2)}) collective-permute-start(bf16[576,1152]{1,0:T(8,128)(2,1)} %dynamic-slice_bitcast_fusion.3), channel_id=1, source_target_pairs={{0,2},{2,0},{1,3},{3,1},{4,6},{6,4},{5,7},{7,5}} | collective-permute-start | bytes 3981320 | tf_op jit(solution)/shard_map/ppermute | solution.py:380
  361.0 152.1 %collective-permute-start.7 = (bf16[576,1152]{1,0:T(8,128)(2,1)}, bf16[576,1152]{1,0:T(8,128)(2,1)}, u32[]{:S(2)}, u32[]{:S(2)}) collective-permute-start(bf16[576,1152]{1,0:T(8,128)(2,1)} %dynamic-slice_bitcast_fusion.2), channel_id=1, source_target_pairs={{0,2},{2,0},{1,3},{3,1},{4,6},{6,4},{5,7},{7,5}} | collective-permute-start | bytes 3981320 | tf_op jit(solution)/shard_map/ppermute | solution.py:380
  502.6 3.4 copy-start.23
  502.6 3.4 copy-start.26
  502.6 3.4 copy-start.48
  503.9 6.1 %copy-start.41 = (f32[16,1152]{1,0:T(8,128)}, f32[16,1152]{1,0:T(8,128)S(1)}, u32[]{:S(2)}) copy-start(f32[16,1152]{1,0:T(8,128)S(1)} %reduce_sum.241) | copy-start | bytes 221188
  506.0 4.0 copy-start.28
  510.0 3.1 copy-start.27
  517.3 13.5 %slice-start = ((s8[10027008]{0:T(1024)(128)(4,1)}), s8[4194304]{0:T(1024)(128)(4,1)S(1)}, s32[]{:S(2)}) async-start(s8[10027008]{0:T(1024)(128)(4,1)} %bitcast.229), calls=%async_computation.13 | async-start | bytes 8388608
  518.8 12.0 %slice-start.1 = ((s8[10027008]{0:T(1024)(128)(4,1)}), s8[4194304]{0:T(1024)(128)(4,1)S(1)}, s32[]{:S(2)}) async-start(s8[10027008]{0:T(1024)(128)(4,1)} %bitcast.229), calls=%async_computation.14 | async-start | bytes 8388608
  518.8 12.0 %slice-start.2 = ((s8[10027008]{0:T(1024)(128)(4,1)}), s8[1638400]{0:T(1024)(128)(4,1)S(1)}, s32[]{:S(2)}) async-start(s8[10027008]{0:T(1024)(128)(4,1)} %bitcast.229), calls=%async_computation.15 | async-start | bytes 3276800
  518.9 12.0 %copy-start.7 = (bf16[4,3,72,2048]{3,2,1,0:T(8,128)(2,1)S(1)}, bf16[4,3,72,2048]{3,2,1,0:T(8,128)(2,1)}, u32[]{:S(2)}) copy-start(bf16[4,3,72,2048]{3,2,1,0:T(8,128)(2,1)} %get-tuple-element.73) | copy-start | bytes 10616836
  530.8 17.2 %copy-start.39 = (bf16[1,2,2,2,72,128]{5,4,3,2,1,0:T(8,128)(2,1)S(1)}, bf16[1,2,2,2,72,128]{5,4,3,2,1,0:T(8,128)(2,1)}, u32[]{:S(2)}) copy-start(bf16[1,2,2,2,72,128]{5,4,3,2,1,0:T(8,128)(2,1)} %reduce-scatter.5.cloned.1.call-done) | copy-start | bytes 442372
  530.9 19.6 %slice-start.3 = ((f32[16,1152]{1,0:T(8,128)}), f32[3,1152]{1,0:T(4,128)S(1)}, s32[]{:S(2)}) async-start(f32[16,1152]{1,0:T(8,128)} %copy-done.41), calls=%async_computation.16 | async-start | bytes 36864 | tf_op jit(solution)/shard_map/slice | solution.py:552
  548.3 5.1 copy-start.20
  (27 other events, 36.5 us)
Sparse Core Ops, SparseCore 0:
  15.6 58.4 all-gather.15
  76.4 70.5 all-gather.13
  148.6 38.1 all-gather.9
  188.2 37.9 all-gather.7
  227.9 46.8 all-gather.11
  325.0 27.5 reduce-scatter.4
  356.5 45.5 reduce-scatter.6
  406.1 45.4 reduce-scatter.8
  504.8 39.7 reduce-scatter.10
